TPU v7x, 128 devices: a whole 4x4x4 slice. The times are simulated.
128 devices in a mesh: chord: 8 (over y_lo, z), span: 16 (over x, y_hi, core).
Axes of the slice: x: 4, y: 4 (y_hi: 2, y_lo: 2; y = y_hi * 2 + y_lo), z: 4, core: 2. Of those that a mesh axis runs over, the one named last changes fastest.
Arguments:
- state: float32 [5, 125, 32, 32, 128], P(None, None, 'chord', 'span'), may hold values from -10 to 10
Outputs:
- residual: float32 [5, 125, 32, 32, 128], P(None, None, 'chord', 'span')
- viscosity: float32 [125, 32, 32, 128], P(None, 'chord', 'span')
All inputs are finite; a program needn't handle non-finite values.
Results may differ from a plain program's by a relative error of at most 0.0001.
Values sent between devices are 32-bit elements; how exact they have to be, the bound alone decides.
A program may use at most 128 MiB of HBM per device.

v0:
```python
import functools
import math

import jax
import jax.numpy as jnp
import numpy as np
from jax import lax
from jax.experimental import pallas as pl
from jax.experimental.pallas import tpu as pltpu
from jax.sharding import PartitionSpec as P

VMEM_BYTES = 52_500_000
EPS_SCALE = 0.01
SENSOR_CENTRE = -3.0
SENSOR_WIDTH = 1.5
RATIO_FLOOR = 1e-06
ENERGY_EPS = 1e-06
GAUSS_NODES = [-0.906179845938664, -0.5384693101056831, 0.0, 0.5384693101056831, 0.906179845938664]
GAUSS_WEIGHTS = [
    0.2369268850561891,
    0.4786286704993665,
    0.5688888888888889,
    0.4786286704993665,
    0.2369268850561891,
]


def legendre_values(points):
    values = [np.ones(points.shape), np.array(points)]
    for order in range(1, 5):
        values.append(
            ((2 * order + 1) * points * values[order] - order * values[order - 1]) / (order + 1)
        )
    return values


def line_tables():
    line_nodes = np.array(GAUSS_NODES)
    quadrature_weights = np.array(GAUSS_WEIGHTS)
    barycentric = np.array(
        [
            1.0 / np.prod([line_nodes[j] - line_nodes[k] for k in range(5) if k != j])
            for j in range(5)
        ]
    )
    derivative = np.zeros((5, 5))
    for i in range(5):
        for j in range(5):
            if i != j:
                derivative[i, j] = barycentric[j] / barycentric[i] / (line_nodes[i] - line_nodes[j])
        derivative[i, i] = -np.sum(derivative[i])
    left_values = np.ones(5)
    right_values = np.ones(5)
    for j in range(5):
        for k in range(5):
            if k != j:
                left_values[j] *= (-1.0 - line_nodes[k]) / (line_nodes[j] - line_nodes[k])
                right_values[j] *= (1.0 - line_nodes[k]) / (line_nodes[j] - line_nodes[k])
    legendre = legendre_values(line_nodes)
    fourth_slope = 7.0 * legendre[3] + 3.0 * legendre[1]
    fifth_slope = 9.0 * legendre[4] + 5.0 * legendre[2] + legendre[0]
    left_corr = 0.5 * (fourth_slope - fifth_slope)
    right_corr = 0.5 * (fourth_slope + fifth_slope)
    modal = np.zeros((5, 5))
    for k in range(5):
        modal[k, :] = quadrature_weights * math.sqrt((2 * k + 1) / 2.0) * legendre[k]
    return (line_nodes, derivative, left_values, right_values, left_corr, right_corr, modal)


NODES, DERIV, LEFT, RIGHT, LIFT_LEFT, LIFT_RIGHT, MODAL = line_tables()
HALF_LEFT = 0.5 * LIFT_LEFT
HALF_RIGHT = 0.5 * LIFT_RIGHT


def fold(u):
    return (u[0] + u[4], u[1] + u[3], u[2], u[0] - u[4], u[1] - u[3])


def traces(parts):
    s0, s1, mid, d0, d1 = parts
    r = [float(x) for x in RIGHT]
    even = 0.5 * (r[0] + r[4]) * s0 + 0.5 * (r[1] + r[3]) * s1 + r[2] * mid
    odd = 0.5 * (r[0] - r[4]) * d0 + 0.5 * (r[1] - r[3]) * d1
    return even - odd, even + odd


def slope(parts, before, after):
    s0, s1, mid, d0, d1 = parts
    h = [float(x) for x in HALF_LEFT]
    r = [float(x) for x in RIGHT]
    if before is not None:
        diff, both = before - after, before + after
    even, odd = [], []
    for i in range(3):
        lift = 0.5 * (h[i] + h[4 - i])
        value = (
            float(0.5 * (DERIV[i, 0] - DERIV[i, 4]) + lift * (r[0] - r[4])) * d0
            + float(0.5 * (DERIV[i, 1] - DERIV[i, 3]) + lift * (r[1] - r[3])) * d1
        )
        even.append(value if before is None else value + lift * diff)
    for i in range(2):
        lift = 0.5 * (h[i] - h[4 - i])
        value = (
            float(0.5 * (DERIV[i, 0] + DERIV[i, 4]) - lift * (r[0] + r[4])) * s0
            + float(0.5 * (DERIV[i, 1] + DERIV[i, 3]) - lift * (r[1] + r[3])) * s1
            + float(DERIV[i, 2] - 2.0 * lift * r[2]) * mid
        )
        odd.append(value if before is None else value + lift * both)
    return [even[0] + odd[0], even[1] + odd[1], even[2], even[1] - odd[1], even[0] - odd[0]]


def points(axis, q, j):
    if axis == 0:
        return [25 * i + 5 * q + j for i in range(5)]
    if axis == 1:
        return [25 * q + 5 * i + j for i in range(5)]
    return [25 * q + 5 * j + i for i in range(5)]


def modal_line(u):
    s0, s1, mid, d0, d1 = fold(u)
    out = []
    for k in range(5):
        m = [float(x) for x in MODAL[k]]
        out.append(m[0] * s0 + m[1] * s1 + m[2] * mid if k % 2 == 0 else m[0] * d0 + m[1] * d1)
    return out


def sensor(load, work):
    def first(q, carry):
        for j in range(5):
            pts = points(0, q, j)
            for i, value in zip(pts, modal_line([load(p) for p in pts])):
                work[i] = value
        return carry

    lax.fori_loop(0, 5, first, 0)

    def second(q, carry):
        total, high = carry
        plane = {}
        for c in range(5):
            for b, value in enumerate(modal_line([work[25 * q + 5 * b + c] for b in range(5)])):
                plane[b, c] = value
        low = jnp.zeros_like(total)
        edge = jnp.zeros_like(total)
        for b in range(5):
            line = modal_line([plane[b, c] for c in range(5)])
            squares = [x * x for x in line]
            if b < 4:
                low = low + ((squares[0] + squares[1]) + (squares[2] + squares[3]))
                edge = edge + squares[4]
            else:
                edge = edge + ((squares[0] + squares[1]) + (squares[2] + squares[3])) + squares[4]
        plane_total = low + edge
        return total + plane_total, high + jnp.where(q == 4, plane_total, edge)

    zero = jnp.zeros(work.shape[1:], jnp.float32)
    total, high = lax.fori_loop(0, 5, second, (zero, zero))
    level = jnp.log(jnp.maximum(high / (total + ENERGY_EPS), RATIO_FLOOR)) * (1.0 / math.log(10.0))
    ramp = jnp.clip((level - SENSOR_CENTRE) / SENSOR_WIDTH, -1.0, 1.0)
    return EPS_SCALE * 0.5 * (1.0 + jnp.sin(0.5 * math.pi * ramp))


def rolled(value, shift, axis):
    size = value.shape[axis]
    return pltpu.roll(value, shift % size, axis)


LOWER = [float((1.0 - x) / 2.0) for x in NODES]
UPPER = [float((1.0 + x) / 2.0) for x in NODES]


def along_lanes(line):
    lanes = line.shape[1]
    lane = lax.broadcasted_iota(jnp.int32, line.shape, 1)
    before = jnp.where(lane == 0, 0.0, rolled(line, 1, 1))
    after = jnp.where(lane == lanes - 1, 0.0, rolled(line, -1, 1))
    return jnp.maximum(line, before), jnp.maximum(line, after)


def interpolate(neighbours, nu):
    corner = {}
    for x in range(2):
        for y in range(2):
            line = jnp.maximum(
                jnp.maximum(neighbours[x][y], neighbours[x + 1][y]),
                jnp.maximum(neighbours[x][y + 1], neighbours[x + 1][y + 1]),
            )
            corner[x, y, 0], corner[x, y, 1] = along_lanes(line)
    lower, upper = LOWER, UPPER
    for a in range(5):
        face = {
            (y, z): lower[a] * corner[0, y, z] + upper[a] * corner[1, y, z]
            for y in range(2)
            for z in range(2)
        }
        for b in range(5):
            edge = [lower[b] * face[0, z] + upper[b] * face[1, z] for z in range(2)]
            for c in range(5):
                nu[25 * a + 5 * b + c] = lower[c] * edge[0] + upper[c] * edge[1]
    return corner


def row_masks(axis, chords, spans, lanes):
    row = lax.broadcasted_iota(jnp.int32, (chords * spans, lanes), 0)
    if axis == 0:
        return row < spans, row >= (chords - 1) * spans
    place = row % spans
    return place == 0, place == spans - 1


def outer_rows(axis, chords, spans, last):
    if axis == 0:
        return pl.ds((chords - 1) * spans if last else 0, spans)
    return pl.ds(spans - 1 if last else 0, chords, spans)


def store_pair(work, slot, left, right, down, up, index, rows_low, rows_high):
    work[2 * slot] = left
    work[2 * slot + 1] = right
    down[index] = work[2 * slot, rows_low]
    up[index] = work[2 * slot + 1, rows_high]


def local_kernel(sizes, count, chords, spans, *refs):
    state_hbm = refs[0]
    nu, acc = refs[1:3]
    (
        state, grad, around, work, eps_out, faces_c, faces_s, gain, edge, beta, outside, alpha,
        t0, t1, t2, t3, f0, f1, f2, f3,
    ) = refs[3:23]
    ghosts, flux_ghosts = refs[23:27], refs[27:31]
    load_sem, eps_send, eps_recv, send_sem, recv_sem = refs[31:]
    sends = ((t0, t1, t2, t3), (f0, f1, f2, f3))
    lands = (ghosts, flux_ghosts)
    rows, lanes = nu.shape[1:]
    chord_size, span_size = sizes
    me_c, me_s = lax.axis_index("chord"), lax.axis_index("span")
    mesh_id = pl.DeviceIdType.MESH

    def load(v):
        return pltpu.make_async_copy(state_hbm.at[v], state.at[v], load_sem.at[v])

    for v in range(count):
        load(v).start()

    def reachable(dx):
        if dx == 0:
            return None
        return me_c + 1 < chord_size if dx == 1 else me_c > 0

    def guarded(cond, run):
        if cond is None:
            run()
        else:
            pl.when(cond)(run)

    def partner(dx, dy):
        return (me_c + dx, lax.rem(me_s + dy + span_size, span_size))

    offsets = [(dx, dy) for dx in (0, -1, 1) for dy in (-1, 0, 1) if (dx, dy) != (0, 0)]
    barrier = pltpu.get_barrier_semaphore()
    for dx, dy in offsets:

        def greet(dx=dx, dy=dy):
            pl.semaphore_signal(barrier, inc=1, device_id=partner(dx, dy), device_id_type=mesh_id)

        guarded(reachable(dx), greet)

    def eps_copy(dx, dy):
        slot = 3 * (dx + 1) + dy + 1
        return pltpu.make_async_remote_copy(
            src_ref=eps_out, dst_ref=around.at[1 - dx, 1 - dy],
            send_sem=eps_send.at[slot], recv_sem=eps_recv.at[8 - slot],
            device_id=partner(dx, dy), device_id_type=mesh_id,
        )

    ways = ((1, 0), (-1, 0), (0, 1), (0, -1))

    def message(stage, k, v):
        dx, dy = ways[k]
        return pltpu.make_async_remote_copy(
            src_ref=sends[stage][k].at[v], dst_ref=lands[stage][k].at[v],
            send_sem=send_sem.at[stage, k, v], recv_sem=recv_sem.at[stage, k, v],
            device_id=partner(dx, dy), device_id_type=mesh_id,
        )

    def launch(stage, axis, v):
        for k in (2 * axis, 2 * axis + 1):
            guarded(reachable(ways[k][0]), lambda k=k: message(stage, k, v).start())

    masks = [row_masks(axis, chords, spans, lanes) for axis in range(2)]
    outer = [[outer_rows(axis, chords, spans, last) for last in (False, True)] for axis in range(2)]

    def send_traces(axis, v):
        up, down = sends[0][2 * axis], sends[0][2 * axis + 1]
        faces = (faces_c, faces_s)[axis]

        def body(q, carry):
            for j in range(5):
                left, right = traces(fold([state[v, p] for p in points(axis, q, j)]))
                faces[v, 5 * q + j] = jnp.where(masks[axis][0], left, right)
                store_pair(work, j, left, right, down, up, (v, 5 * q + j), *outer[axis])
            return carry

        lax.fori_loop(0, 5, body, 0)

    load(0).wait()
    send_traces(1, 0)
    sides = jnp.where(me_c > 0, 1, 0) + jnp.where(me_c + 1 < chord_size, 1, 0)
    pl.semaphore_wait(barrier, 2 + 3 * sides)
    launch(0, 1, 0)
    eps = sensor(lambda p: state[0, p], work)
    eps_out[...] = eps
    around[1, 1] = eps
    for dx, dy in offsets:
        guarded(reachable(dx), lambda dx=dx, dy=dy: eps_copy(dx, dy).start())

    send_traces(0, 0)
    launch(0, 0, 0)

    def later_traces(v, carry):
        load(v).wait()
        for axis in (1, 0):
            send_traces(axis, v)
            launch(0, axis, v)
        return carry

    lax.fori_loop(1, count, later_traces, 0)

    lane = lax.broadcasted_iota(jnp.int32, (rows, lanes), 1)
    first, last = lane == 0, lane == lanes - 1

    def normal_gradient(v, carry):
        def body(q, carry):
            for j in range(5):
                pts = points(2, q, j)
                parts = fold([state[v, p] for p in pts])
                left, right = traces(parts)
                before = jnp.where(first, left, rolled(right, 1, 1))
                after = jnp.where(last, right, rolled(left, -1, 1))
                for p, value in zip(pts, slope(parts, before, after)):
                    grad[v, p] = value
            return carry

        lax.fori_loop(0, 5, body, 0, unroll=True)
        return carry

    lax.fori_loop(0, count, normal_gradient, 0)

    row = lax.broadcasted_iota(jnp.int32, (rows, lanes), 0)
    for dx, dy in offsets:
        guarded(reachable(-dx), lambda dx=dx, dy=dy: eps_copy(dx, dy).wait_recv())

    have_low = jnp.where(me_c > 0, spans, 0)
    have_high = jnp.where(me_c + 1 < chord_size, rows, rows - spans)
    low_s, high_s = masks[1]
    low_c, high_c = masks[0]
    column = []
    for x in range(3):
        mine, left, right = around[x, 1], around[x, 0], around[x, 2]
        column.append([
            jnp.where(low_s, rolled(left, 1 - spans, 0), rolled(mine, 1, 0)),
            mine,
            jnp.where(high_s, rolled(right, spans - 1, 0), rolled(mine, -1, 0)),
            jnp.where(low_s, rolled(left, 2 - spans, 0), rolled(right, spans - 2, 0)),
        ])
    closed_low = row < spans - have_low
    closed_high = row >= have_high
    neighbours = [[], [], [], []]
    for y in range(4):
        inner = column[1][y]
        below = jnp.where(low_c, rolled(column[0][y], spans, 0), rolled(inner, spans, 0))
        above = jnp.where(high_c, rolled(column[2][y], -spans, 0), rolled(inner, -spans, 0))
        beyond = jnp.where(
            low_c, rolled(column[0][y], 2 * spans, 0), rolled(column[2][y], -2 * spans, 0)
        )
        neighbours[0].append(jnp.where(closed_low, 0.0, below))
        neighbours[1].append(inner)
        neighbours[2].append(jnp.where(closed_high, 0.0, above))
        neighbours[3].append(beyond)
    corner = interpolate(neighbours, nu)
    near_weight = sum(float(LEFT[i] * HALF_LEFT[i] * (1.0 - NODES[i]) / 2.0) for i in range(5))
    far_weight = sum(float(LEFT[i] * HALF_LEFT[i] * (1.0 + NODES[i]) / 2.0) for i in range(5))
    for axis in range(2):
        low = masks[axis][0]
        sign = jnp.where(low, -1.0, 1.0)
        weight = {}
        for t in range(2):
            pair = []
            for o in (t, t + 1):
                if axis == 0:
                    pair += [jnp.where(low, neighbours[0][o], neighbours[2][o]), neighbours[3][o]]
                else:
                    pair += [jnp.where(low, neighbours[o][0], neighbours[o][2]), neighbours[o][3]]
            line = jnp.maximum(jnp.maximum(pair[0], pair[1]), jnp.maximum(pair[2], pair[3]))
            far = along_lanes(line)
            for z in range(2):
                if axis == 0:
                    near = jnp.where(low, corner[0, t, z], corner[1, t, z])
                else:
                    near = jnp.where(low, corner[t, 0, z], corner[t, 1, z])
                weight[t, z] = sign * (near_weight * near + far_weight * far[z])
        for m in range(5):
            ends = [LOWER[m] * weight[0, z] + UPPER[m] * weight[1, z] for z in range(2)]
            for c in range(5):
                beta[axis, 5 * m + c] = LOWER[c] * ends[0] + UPPER[c] * ends[1]

    for axis in (1, 0):

        def variable(v, carry):
            up, down = sends[1][2 * axis], sends[1][2 * axis + 1]
            low, high = masks[axis]
            step = spans if axis == 0 else 1

            def body(q, carry):
                for j in range(5):
                    pts = points(axis, q, j)
                    parts = fold([state[v, p] for p in pts])
                    left, right = traces(parts)
                    before = jnp.where(low, 0.0, rolled(right, step, 0))
                    after = jnp.where(high, 0.0, rolled(left, -step, 0))
                    if axis == 0:
                        before = jnp.where(closed_low, left, before)
                        after = jnp.where(closed_high, right, after)
                    gradient = slope(parts, before, after)
                    parts = fold([nu[p] * g for p, g in zip(pts, gradient)])
                    left, right = traces(parts)
                    store_pair(work, j, left, right, down, up, (v, 5 * q + j), *outer[axis])
                    before = jnp.where(low, 0.0, rolled(right, step, 0))
                    after = jnp.where(high, 0.0, rolled(left, -step, 0))
                    if axis == 0:
                        before = jnp.where(closed_low, -left, before)
                        after = jnp.where(closed_high, -right, after)
                    for p, value in zip(pts, slope(parts, before, after)):
                        if axis == 1:
                            acc[v, p] = value
                        else:
                            acc[v, p] += value
                return carry

            lax.fori_loop(0, 5, body, 0, unroll=True)
            launch(1, axis, v)
            return carry

        lax.fori_loop(0, count, variable, 0)

    for axis in range(2):
        low, high = masks[axis]

        def gains(q, carry):
            for j in range(5):
                f = 5 * q + j
                spread = []
                for i, p in enumerate(points(axis, q, j)):
                    lift = jnp.where(high, float(HALF_RIGHT[i]), 0.0)
                    spread.append(nu[p] * jnp.where(low, float(HALF_LEFT[i]), lift))
                parts = fold(spread)
                left, right = traces(parts)
                edge[axis, 2 * f] = left
                edge[axis, 2 * f + 1] = right
                for i, value in enumerate(slope(parts, None, None)):
                    gain[axis, 5 * f + i] = value
            return carry

        lax.fori_loop(0, 5, gains, 0)

    def normal(v, carry):
        def body(q, carry):
            for j in range(5):
                pts = points(2, q, j)
                parts = fold([nu[p] * grad[v, p] for p in pts])
                left, right = traces(parts)
                before = jnp.where(first, -left, rolled(right, 1, 1))
                after = jnp.where(last, -right, rolled(left, -1, 1))
                for p, value in zip(pts, slope(parts, before, after)):
                    acc[v, p] += value
            return carry

        lax.fori_loop(0, 5, body, 0, unroll=True)
        return carry

    lax.fori_loop(0, count, normal, 0)

    def arrived(axis, v):
        for k in (2 * axis, 2 * axis + 1):
            for stage in range(2):
                guarded(
                    reachable(-ways[k][0]),
                    lambda k=k, stage=stage: message(stage, k, v).wait_recv(),
                )

    for axis in (0, 1):

        def correct(v, carry):
            arrived(axis, v)
            up, down = ghosts[2 * axis], ghosts[2 * axis + 1]
            f_up, f_down = flux_ghosts[2 * axis], flux_ghosts[2 * axis + 1]
            faces = (faces_c, faces_s)[axis]
            low, high = masks[axis]
            rows_low, rows_high = outer[axis]
            step = spans if axis == 0 else 1
            opened = low | high
            if axis == 0:
                opened = opened & jnp.logical_not(closed_low | closed_high)

            def gather(q, carry):
                for j in range(5):
                    f = 5 * q + j
                    outside[f, rows_low] = up[v, f]
                    outside[f, rows_high] = down[v, f]
                    alpha[f, rows_low] = f_up[v, f]
                    alpha[f, rows_high] = f_down[v, f]
                return carry

            lax.fori_loop(0, 5, gather, 0)

            def body(q, carry):
                for j in range(5):
                    f = 5 * q + j
                    ghost = jnp.where(opened, outside[f], 0.0)
                    flux = jnp.where(opened, alpha[f] + beta[axis, f] * faces[v, f], 0.0)
                    before = jnp.where(low, flux, rolled(edge[axis, 2 * f + 1] * ghost, step, 0))
                    after = jnp.where(high, flux, rolled(edge[axis, 2 * f] * ghost, -step, 0))
                    h = [float(x) for x in HALF_LEFT]
                    diff, both = before - after, before + after
                    even = [0.5 * (h[i] + h[4 - i]) * diff for i in range(3)]
                    odd = [0.5 * (h[i] - h[4 - i]) * both for i in range(2)]
                    lifts = [
                        even[0] + odd[0], even[1] + odd[1], even[2],
                        even[1] - odd[1], even[0] - odd[0],
                    ]
                    for i, p in enumerate(points(axis, q, j)):
                        acc[v, p] += gain[axis, 5 * f + i] * ghost + lifts[i]
                return carry

            lax.fori_loop(0, 5, body, 0, unroll=True)
            return carry

        lax.fori_loop(0, count, correct, 0)

    for dx, dy in offsets:
        guarded(reachable(dx), lambda dx=dx, dy=dy: eps_copy(dx, dy).wait_send())
    for stage in range(2):
        for k in range(4):
            for v in range(count):
                guarded(
                    reachable(ways[k][0]),
                    lambda stage=stage, k=k, v=v: message(stage, k, v).wait_send(),
                )


def shards(state):
    count, npts, chords, spans, lanes = state.shape
    rows = chords * spans
    flat = state.reshape(count, npts, rows, lanes)
    f32 = jnp.float32
    sizes = (lax.axis_size("chord"), lax.axis_size("span"))

    def message(n, k):
        return (n, 25, spans if k < 2 else chords, lanes)

    def full(*shape):
        return jax.ShapeDtypeStruct(shape, f32)

    vmem = pl.BlockSpec(memory_space=pltpu.VMEM)
    nu, residual = pl.pallas_call(
        functools.partial(local_kernel, sizes, count, chords, spans),
        in_specs=[pl.BlockSpec(memory_space=pltpu.HBM)],
        out_specs=[vmem, vmem],
        out_shape=[full(npts, rows, lanes), full(count, npts, rows, lanes)],
        scratch_shapes=[
            pltpu.VMEM(shape, f32)
            for shape in [
                (count, npts, rows, lanes),
                (count, npts, rows, lanes),
                (3, 3, rows, lanes),
                (npts, rows, lanes),
                (rows, lanes),
                (count, 25, rows, lanes),
                (count, 25, rows, lanes),
                (2, npts, rows, lanes),
                (2, 50, rows, lanes),
                (2, 25, rows, lanes),
                (25, rows, lanes),
                (25, rows, lanes),
            ]
            + [message(count, k) for k in range(4)] * 4
        ]
        + [
            pltpu.SemaphoreType.DMA((count,)),
            pltpu.SemaphoreType.DMA((9,)),
            pltpu.SemaphoreType.DMA((9,)),
            pltpu.SemaphoreType.DMA((2, 4, count)),
            pltpu.SemaphoreType.DMA((2, 4, count)),
        ],
        compiler_params=pltpu.CompilerParams(
            collective_id=0, has_side_effects=True, vmem_limit_bytes=VMEM_BYTES
        ),
    )(flat)
    return residual.reshape(state.shape), nu.reshape(npts, chords, spans, lanes)


def solution(mesh):
    in_specs = (P(None, None, "chord", "span", None),)
    out_specs = (P(None, None, "chord", "span", None), P(None, "chord", "span", None))
    return jax.shard_map(shards, mesh=mesh, in_specs=in_specs, out_specs=out_specs, check_vma=False)
```

profile of v0, /device:TPU:9, one launch (start us, length us, event | category | flops | bytes accessed | tf_op | source)
XLA Modules:
  0.0 30.1 jit_solution(13041441107397230179)
XLA Ops:
  0.6 27.2 %shard_map.30 = (f32[125,8,128]{2,1,0:T(8,128)S(1)}, f32[5,125,8,128]{3,2,1,0:T(8,128)S(1)}) custom-call(f32[5,125,8,128]{3,2,1,0:T(8,128)} %bitcast.5), custom_call_target="tpu_custom_call" | custom-call | tf_op jit(solution)/shard_map/pallas_call | solution.py:568
  27.8 1.5 %copy.5 = f32[5,125,4,2,128]{4,3,2,1,0:T(2,128)} copy(f32[5,125,4,2,128]{4,3,2,1,0:T(2,128)S(1)} %bitcast.3) | data formatting | bytes 5120000
  29.3 0.8 %copy.6 = f32[125,4,2,128]{3,2,1,0:T(2,128)} copy(f32[125,4,2,128]{3,2,1,0:T(2,128)S(1)} %bitcast.4) | data formatting | bytes 1024000
where the time goes:
time: 30.2 us; the launch traced here: 30.1 us
  Pallas kernels  27.2 us (90%)
  local copies, waits for them, and re-layouts  2.26 us (7%)
  between operations  0.64 us (2%)
    pallas_call x1, Pallas kernels, shards(): pl.pallas_call(functools.partial(local_kernel, sizes, count, chords, span...  27.2 us
    unnamed x2, local copies, waits for them, and re-layouts  2.26 us

commit v1 on v0

--- a/solution.py
+++ b/solution.py
@@ -199,7 +199,6 @@
             edge = [lower[b] * face[0, z] + upper[b] * face[1, z] for z in range(2)]
             for c in range(5):
                 nu[25 * a + 5 * b + c] = lower[c] * edge[0] + upper[c] * edge[1]
-    return corner
 
 
 def row_masks(axis, chords, spans, lanes):
@@ -216,22 +215,20 @@
     return pl.ds(spans - 1 if last else 0, chords, spans)
 
 
-def store_pair(work, slot, left, right, down, up, index, rows_low, rows_high):
-    work[2 * slot] = left
-    work[2 * slot + 1] = right
-    down[index] = work[2 * slot, rows_low]
-    up[index] = work[2 * slot + 1, rows_high]
+def weights(axis, masks):
+    low, high = masks[axis]
+    return [
+        jnp.where(low, float(HALF_LEFT[i]), jnp.where(high, float(HALF_RIGHT[i]), 0.0))
+        for i in range(5)
+    ]
 
 
 def local_kernel(sizes, count, chords, spans, *refs):
     state_hbm = refs[0]
     nu, acc = refs[1:3]
-    (
-        state, grad, around, work, eps_out, faces_c, faces_s, gain, edge, beta, outside, alpha,
-        t0, t1, t2, t3, f0, f1, f2, f3,
-    ) = refs[3:23]
-    ghosts, flux_ghosts = refs[23:27], refs[27:31]
-    load_sem, eps_send, eps_recv, send_sem, recv_sem = refs[31:]
+    state, grad, around, work, eps_out, faces, outside, lifted, t0, t1, t2, t3, f0, f1, f2, f3 = refs[3:19]
+    ghosts, flux_ghosts = refs[19:23], refs[23:27]
+    load_sem, eps_send, eps_recv, send_sem, recv_sem = refs[27:]
     sends = ((t0, t1, t2, t3), (f0, f1, f2, f3))
     lands = (ghosts, flux_ghosts)
     rows, lanes = nu.shape[1:]
@@ -239,12 +236,6 @@
     me_c, me_s = lax.axis_index("chord"), lax.axis_index("span")
     mesh_id = pl.DeviceIdType.MESH
 
-    def load(v):
-        return pltpu.make_async_copy(state_hbm.at[v], state.at[v], load_sem.at[v])
-
-    for v in range(count):
-        load(v).start()
-
     def reachable(dx):
         if dx == 0:
             return None
@@ -267,6 +258,12 @@
             pl.semaphore_signal(barrier, inc=1, device_id=partner(dx, dy), device_id_type=mesh_id)
 
         guarded(reachable(dx), greet)
+
+    def load(v):
+        return pltpu.make_async_copy(state_hbm.at[v], state.at[v], load_sem.at[v])
+
+    for v in range(count):
+        load(v).start()
 
     def eps_copy(dx, dy):
         slot = 3 * (dx + 1) + dy + 1
@@ -282,47 +279,78 @@
         dx, dy = ways[k]
         return pltpu.make_async_remote_copy(
             src_ref=sends[stage][k].at[v], dst_ref=lands[stage][k].at[v],
-            send_sem=send_sem.at[stage, k, v], recv_sem=recv_sem.at[stage, k, v],
+            send_sem=send_sem.at[stage, k], recv_sem=recv_sem.at[stage, k, v],
             device_id=partner(dx, dy), device_id_type=mesh_id,
         )
 
+    def sent(stage, k):
+        dx, dy = ways[k]
+        return pltpu.make_async_remote_copy(
+            src_ref=sends[stage][k], dst_ref=lands[stage][k],
+            send_sem=send_sem.at[stage, k], recv_sem=recv_sem.at[stage, k, 0],
+            device_id=partner(dx, dy), device_id_type=mesh_id,
+        )
+
     def launch(stage, axis, v):
+        sign = 1.0 if stage == 0 else -1.0
         for k in (2 * axis, 2 * axis + 1):
             guarded(reachable(ways[k][0]), lambda k=k: message(stage, k, v).start())
+        if axis == 0:
+            for k in range(2):
+
+                def mirror(k=k):
+                    lands[stage][1 - k][v] = sign * sends[stage][k][v]
+
+                pl.when(jnp.logical_not(reachable(ways[k][0])))(mirror)
+
+    def arrived(stage, axis, v):
+        for k in (2 * axis, 2 * axis + 1):
+            guarded(reachable(-ways[k][0]), lambda k=k: message(stage, k, v).wait_recv())
 
     masks = [row_masks(axis, chords, spans, lanes) for axis in range(2)]
     outer = [[outer_rows(axis, chords, spans, last) for last in (False, True)] for axis in range(2)]
 
+    def extract(stage, axis, v, f, ref, index):
+        up, down = sends[stage][2 * axis], sends[stage][2 * axis + 1]
+        down[v, f] = ref[index + (outer[axis][0],)]
+        up[v, f] = ref[index[:-1] + (index[-1] + 1, outer[axis][1])]
+
+    def gather(stage, axis, v, f, ref):
+        up, down = lands[stage][2 * axis], lands[stage][2 * axis + 1]
+        ref[axis, f, outer[axis][0]] = up[v, f]
+        ref[axis, f, outer[axis][1]] = down[v, f]
+        return ref[axis, f]
+
     def send_traces(axis, v):
-        up, down = sends[0][2 * axis], sends[0][2 * axis + 1]
-        faces = (faces_c, faces_s)[axis]
-
         def body(q, carry):
             for j in range(5):
+                f = 5 * q + j
                 left, right = traces(fold([state[v, p] for p in points(axis, q, j)]))
-                faces[v, 5 * q + j] = jnp.where(masks[axis][0], left, right)
-                store_pair(work, j, left, right, down, up, (v, 5 * q + j), *outer[axis])
+                faces[axis, v, 2 * f] = left
+                faces[axis, v, 2 * f + 1] = right
+                extract(0, axis, v, f, faces, (axis, v, 2 * f))
             return carry
 
         lax.fori_loop(0, 5, body, 0)
 
+    for f in range(25):
+        lifted[0, f] = jnp.zeros((rows, lanes), jnp.float32)
     load(0).wait()
-    send_traces(1, 0)
-    sides = jnp.where(me_c > 0, 1, 0) + jnp.where(me_c + 1 < chord_size, 1, 0)
-    pl.semaphore_wait(barrier, 2 + 3 * sides)
-    launch(0, 1, 0)
     eps = sensor(lambda p: state[0, p], work)
     eps_out[...] = eps
     around[1, 1] = eps
+    send_traces(1, 0)
+    send_traces(0, 0)
+    sides = jnp.where(me_c > 0, 1, 0) + jnp.where(me_c + 1 < chord_size, 1, 0)
+    pl.semaphore_wait(barrier, 2 + 3 * sides)
     for dx, dy in offsets:
         guarded(reachable(dx), lambda dx=dx, dy=dy: eps_copy(dx, dy).start())
-
-    send_traces(0, 0)
     launch(0, 0, 0)
+    launch(0, 1, 0)
 
     def later_traces(v, carry):
         load(v).wait()
-        for axis in (1, 0):
+        for axis in range(2):
             send_traces(axis, v)
             launch(0, axis, v)
         return carry
@@ -364,107 +392,57 @@
             jnp.where(low_s, rolled(left, 1 - spans, 0), rolled(mine, 1, 0)),
             mine,
             jnp.where(high_s, rolled(right, spans - 1, 0), rolled(mine, -1, 0)),
-            jnp.where(low_s, rolled(left, 2 - spans, 0), rolled(right, spans - 2, 0)),
         ])
     closed_low = row < spans - have_low
     closed_high = row >= have_high
-    neighbours = [[], [], [], []]
-    for y in range(4):
+    neighbours = [[], [], []]
+    for y in range(3):
         inner = column[1][y]
         below = jnp.where(low_c, rolled(column[0][y], spans, 0), rolled(inner, spans, 0))
         above = jnp.where(high_c, rolled(column[2][y], -spans, 0), rolled(inner, -spans, 0))
-        beyond = jnp.where(
-            low_c, rolled(column[0][y], 2 * spans, 0), rolled(column[2][y], -2 * spans, 0)
-        )
         neighbours[0].append(jnp.where(closed_low, 0.0, below))
         neighbours[1].append(inner)
         neighbours[2].append(jnp.where(closed_high, 0.0, above))
-        neighbours[3].append(beyond)
-    corner = interpolate(neighbours, nu)
-    near_weight = sum(float(LEFT[i] * HALF_LEFT[i] * (1.0 - NODES[i]) / 2.0) for i in range(5))
-    far_weight = sum(float(LEFT[i] * HALF_LEFT[i] * (1.0 + NODES[i]) / 2.0) for i in range(5))
-    for axis in range(2):
-        low = masks[axis][0]
-        sign = jnp.where(low, -1.0, 1.0)
-        weight = {}
-        for t in range(2):
-            pair = []
-            for o in (t, t + 1):
-                if axis == 0:
-                    pair += [jnp.where(low, neighbours[0][o], neighbours[2][o]), neighbours[3][o]]
-                else:
-                    pair += [jnp.where(low, neighbours[o][0], neighbours[o][2]), neighbours[o][3]]
-            line = jnp.maximum(jnp.maximum(pair[0], pair[1]), jnp.maximum(pair[2], pair[3]))
-            far = along_lanes(line)
-            for z in range(2):
-                if axis == 0:
-                    near = jnp.where(low, corner[0, t, z], corner[1, t, z])
-                else:
-                    near = jnp.where(low, corner[t, 0, z], corner[t, 1, z])
-                weight[t, z] = sign * (near_weight * near + far_weight * far[z])
-        for m in range(5):
-            ends = [LOWER[m] * weight[0, z] + UPPER[m] * weight[1, z] for z in range(2)]
-            for c in range(5):
-                beta[axis, 5 * m + c] = LOWER[c] * ends[0] + UPPER[c] * ends[1]
-
-    for axis in (1, 0):
-
-        def variable(v, carry):
-            up, down = sends[1][2 * axis], sends[1][2 * axis + 1]
-            low, high = masks[axis]
-            step = spans if axis == 0 else 1
-
-            def body(q, carry):
-                for j in range(5):
-                    pts = points(axis, q, j)
-                    parts = fold([state[v, p] for p in pts])
-                    left, right = traces(parts)
-                    before = jnp.where(low, 0.0, rolled(right, step, 0))
-                    after = jnp.where(high, 0.0, rolled(left, -step, 0))
-                    if axis == 0:
-                        before = jnp.where(closed_low, left, before)
-                        after = jnp.where(closed_high, right, after)
-                    gradient = slope(parts, before, after)
-                    parts = fold([nu[p] * g for p, g in zip(pts, gradient)])
-                    left, right = traces(parts)
-                    store_pair(work, j, left, right, down, up, (v, 5 * q + j), *outer[axis])
-                    before = jnp.where(low, 0.0, rolled(right, step, 0))
-                    after = jnp.where(high, 0.0, rolled(left, -step, 0))
-                    if axis == 0:
-                        before = jnp.where(closed_low, -left, before)
-                        after = jnp.where(closed_high, -right, after)
-                    for p, value in zip(pts, slope(parts, before, after)):
-                        if axis == 1:
-                            acc[v, p] = value
-                        else:
-                            acc[v, p] += value
-                return carry
-
-            lax.fori_loop(0, 5, body, 0, unroll=True)
-            launch(1, axis, v)
-            return carry
-
-        lax.fori_loop(0, count, variable, 0)
-
-    for axis in range(2):
+    interpolate(neighbours, nu)
+
+    def flux(axis, v):
         low, high = masks[axis]
-
-        def gains(q, carry):
+        step = spans if axis == 0 else 1
+
+        def body(q, carry):
             for j in range(5):
                 f = 5 * q + j
-                spread = []
-                for i, p in enumerate(points(axis, q, j)):
-                    lift = jnp.where(high, float(HALF_RIGHT[i]), 0.0)
-                    spread.append(nu[p] * jnp.where(low, float(HALF_LEFT[i]), lift))
-                parts = fold(spread)
+                pts = points(axis, q, j)
+                parts = fold([state[v, p] for p in pts])
+                left, right = faces[axis, v, 2 * f], faces[axis, v, 2 * f + 1]
+                ghost = gather(0, axis, v, f, outside)
+                before = jnp.where(low, ghost, rolled(right, step, 0))
+                after = jnp.where(high, ghost, rolled(left, -step, 0))
+                gradient = slope(parts, before, after)
+                parts = fold([nu[p] * g for p, g in zip(pts, gradient)])
                 left, right = traces(parts)
-                edge[axis, 2 * f] = left
-                edge[axis, 2 * f + 1] = right
-                for i, value in enumerate(slope(parts, None, None)):
-                    gain[axis, 5 * f + i] = value
+                work[2 * f] = left
+                work[2 * f + 1] = right
+                extract(1, axis, v, f, work, (2 * f,))
+                before = jnp.where(low, 0.0, rolled(right, step, 0))
+                after = jnp.where(high, 0.0, rolled(left, -step, 0))
+                for p, value in zip(pts, slope(parts, before, after)):
+                    if axis == 0:
+                        acc[v, p] = value
+                    else:
+                        acc[v, p] += value
             return carry
 
-        lax.fori_loop(0, 5, gains, 0)
+        lax.fori_loop(0, 5, body, 0, unroll=True)
+
+    def variable(v, carry):
+        for axis in range(2):
+            arrived(0, axis, v)
+            flux(axis, v)
+            launch(1, axis, v)
+        return carry
+
+    lax.fori_loop(0, count, variable, 0)
 
     def normal(v, carry):
         def body(q, carry):
@@ -483,72 +461,29 @@
 
     lax.fori_loop(0, count, normal, 0)
 
-    def arrived(axis, v):
-        for k in (2 * axis, 2 * axis + 1):
-            for stage in range(2):
-                guarded(
-                    reachable(-ways[k][0]),
-                    lambda k=k, stage=stage: message(stage, k, v).wait_recv(),
-                )
-
-    for axis in (0, 1):
-
-        def correct(v, carry):
-            arrived(axis, v)
-            up, down = ghosts[2 * axis], ghosts[2 * axis + 1]
-            f_up, f_down = flux_ghosts[2 * axis], flux_ghosts[2 * axis + 1]
-            faces = (faces_c, faces_s)[axis]
-            low, high = masks[axis]
-            rows_low, rows_high = outer[axis]
-            step = spans if axis == 0 else 1
-            opened = low | high
-            if axis == 0:
-                opened = opened & jnp.logical_not(closed_low | closed_high)
-
-            def gather(q, carry):
-                for j in range(5):
-                    f = 5 * q + j
-                    outside[f, rows_low] = up[v, f]
-                    outside[f, rows_high] = down[v, f]
-                    alpha[f, rows_low] = f_up[v, f]
-                    alpha[f, rows_high] = f_down[v, f]
-                return carry
-
-            lax.fori_loop(0, 5, gather, 0)
-
-            def body(q, carry):
-                for j in range(5):
-                    f = 5 * q + j
-                    ghost = jnp.where(opened, outside[f], 0.0)
-                    flux = jnp.where(opened, alpha[f] + beta[axis, f] * faces[v, f], 0.0)
-                    before = jnp.where(low, flux, rolled(edge[axis, 2 * f + 1] * ghost, step, 0))
-                    after = jnp.where(high, flux, rolled(edge[axis, 2 * f] * ghost, -step, 0))
-                    h = [float(x) for x in HALF_LEFT]
-                    diff, both = before - after, before + after
-                    even = [0.5 * (h[i] + h[4 - i]) * diff for i in range(3)]
-                    odd = [0.5 * (h[i] - h[4 - i]) * both for i in range(2)]
-                    lifts = [
-                        even[0] + odd[0], even[1] + odd[1], even[2],
-                        even[1] - odd[1], even[0] - odd[0],
-                    ]
-                    for i, p in enumerate(points(axis, q, j)):
-                        acc[v, p] += gain[axis, 5 * f + i] * ghost + lifts[i]
-                return carry
-
-            lax.fori_loop(0, 5, body, 0, unroll=True)
-            return carry
-
-        lax.fori_loop(0, count, correct, 0)
+    weight_c, weight_s = weights(0, masks), weights(1, masks)
+
+    def correct(v, carry):
+        for axis in range(2):
+            arrived(1, axis, v)
+        for f in range(25):
+            for axis in range(2):
+                gather(1, axis, v, f, lifted)
+        for c in range(5):
+            across = [lifted[0, 5 * b + c] for b in range(5)]
+            for a in range(5):
+                along = lifted[1, 5 * a + c]
+                for b in range(5):
+                    acc[v, 25 * a + 5 * b + c] += weight_c[a] * across[b] + weight_s[b] * along
+        return carry
+
+    lax.fori_loop(0, count, correct, 0)
 
     for dx, dy in offsets:
         guarded(reachable(dx), lambda dx=dx, dy=dy: eps_copy(dx, dy).wait_send())
     for stage in range(2):
         for k in range(4):
-            for v in range(count):
-                guarded(
-                    reachable(ways[k][0]),
-                    lambda stage=stage, k=k, v=v: message(stage, k, v).wait_send(),
-                )
+            guarded(reachable(ways[k][0]), lambda stage=stage, k=k: sent(stage, k).wait_send())
 
 
 def shards(state):
@@ -578,13 +513,9 @@
                 (3, 3, rows, lanes),
                 (npts, rows, lanes),
                 (rows, lanes),
-                (count, 25, rows, lanes),
-                (count, 25, rows, lanes),
-                (2, npts, rows, lanes),
-                (2, 50, rows, lanes),
+                (2, count, 50, rows, lanes),
                 (2, 25, rows, lanes),
-                (25, rows, lanes),
-                (25, rows, lanes),
+                (2, 25, rows, lanes),
             ]
             + [message(count, k) for k in range(4)] * 4
         ]
@@ -592,7 +523,7 @@
             pltpu.SemaphoreType.DMA((count,)),
             pltpu.SemaphoreType.DMA((9,)),
             pltpu.SemaphoreType.DMA((9,)),
-            pltpu.SemaphoreType.DMA((2, 4, count)),
+            pltpu.SemaphoreType.DMA((2, 4)),
             pltpu.SemaphoreType.DMA((2, 4, count)),
         ],
         compiler_params=pltpu.CompilerParams(

time: 30.2 us -> 28.7 us (0.950)
  Pallas kernels: 27.2 us -> 25.6 us
    pallas_call x1, Pallas kernels: 27.2 us -> 25.6 us  [shards(): pl.pallas_call(functools.partial(local_kernel, sizes, count, chords, span...]
where the time goes in v1:
time: 28.7 us; the launch traced here: 28.5 us
  Pallas kernels  25.6 us (89%)
  local copies, waits for them, and re-layouts  2.26 us (8%)
  between operations  0.64 us (2%)
    pallas_call x1, Pallas kernels, shards(): pl.pallas_call(functools.partial(local_kernel, sizes, count, chords, span...  25.6 us
    unnamed x2, local copies, waits for them, and re-layouts  2.26 us

profile of v1, /device:TPU:9, one launch (start us, length us, event | category | flops | bytes accessed | tf_op | source)
XLA Modules:
  0.0 28.5 jit_solution(10903244414314926445)
XLA Ops:
  0.6 25.6 %shard_map.30 = (f32[125,8,128]{2,1,0:T(8,128)S(1)}, f32[5,125,8,128]{3,2,1,0:T(8,128)S(1)}) custom-call(f32[5,125,8,128]{3,2,1,0:T(8,128)} %bitcast.5), custom_call_target="tpu_custom_call" | custom-call | tf_op jit(solution)/shard_map/pallas_call | solution.py:503
  26.2 1.5 %copy.5 = f32[5,125,4,2,128]{4,3,2,1,0:T(2,128)} copy(f32[5,125,4,2,128]{4,3,2,1,0:T(2,128)S(1)} %bitcast.3) | data formatting | bytes 5120000
  27.7 0.8 %copy.6 = f32[125,4,2,128]{3,2,1,0:T(2,128)} copy(f32[125,4,2,128]{3,2,1,0:T(2,128)S(1)} %bitcast.4) | data formatting | bytes 1024000

commit v2 on v1

--- a/solution.py
+++ b/solution.py
@@ -226,11 +226,10 @@
 def local_kernel(sizes, count, chords, spans, *refs):
     state_hbm = refs[0]
     nu, acc = refs[1:3]
-    state, grad, around, work, eps_out, faces, outside, lifted, t0, t1, t2, t3, f0, f1, f2, f3 = refs[3:19]
-    ghosts, flux_ghosts = refs[19:23], refs[23:27]
-    load_sem, eps_send, eps_recv, send_sem, recv_sem = refs[27:]
-    sends = ((t0, t1, t2, t3), (f0, f1, f2, f3))
-    lands = (ghosts, flux_ghosts)
+    state, grad, around, work, eps_out, faces, outside, lifted, relay = refs[3:12]
+    sends = (refs[12:16], refs[16:20])
+    lands = (refs[20:24], refs[24:28])
+    load_sem, eps_send, eps_recv, send_sem, recv_sem, relay_sem, pass_sem = refs[28:]
     rows, lanes = nu.shape[1:]
     chord_size, span_size = sizes
     me_c, me_s = lax.axis_index("chord"), lax.axis_index("span")
@@ -250,6 +249,12 @@
     def partner(dx, dy):
         return (me_c + dx, lax.rem(me_s + dy + span_size, span_size))
 
+    cut = chord_size // 2
+    ends = ((cut - 1, 0, cut), (cut, chord_size - 1, cut - 1))
+    twin = me_s + 1 - 2 * lax.rem(me_s, 2)
+    detoured = lax.rem((me_s + 1) // 2, 2) == 1
+    relaying = jnp.logical_not(detoured)
+
     offsets = [(dx, dy) for dx in (0, -1, 1) for dy in (-1, 0, 1) if (dx, dy) != (0, 0)]
     barrier = pltpu.get_barrier_semaphore()
     for dx, dy in offsets:
@@ -258,6 +263,16 @@
             pl.semaphore_signal(barrier, inc=1, device_id=partner(dx, dy), device_id_type=mesh_id)
 
         guarded(reachable(dx), greet)
+
+    for source, through, target in ends:
+        for here, ready, there in ((through, relaying, source), (target, detoured, through)):
+
+            def greet_relay(there=there):
+                pl.semaphore_signal(
+                    barrier, inc=1, device_id=(there, twin), device_id_type=mesh_id
+                )
+
+            pl.when((me_c == here) & ready)(greet_relay)
 
     def load(v):
         return pltpu.make_async_copy(state_hbm.at[v], state.at[v], load_sem.at[v])
@@ -291,10 +306,49 @@
             device_id=partner(dx, dy), device_id_type=mesh_id,
         )
 
+    def detour(stage, k, v):
+        return pltpu.make_async_remote_copy(
+            src_ref=sends[stage][k].at[v], dst_ref=relay.at[stage, v],
+            send_sem=send_sem.at[stage, k], recv_sem=relay_sem.at[stage, v],
+            device_id=(ends[k][1], twin), device_id_type=mesh_id,
+        )
+
+    def onward(stage, k, v):
+        return pltpu.make_async_remote_copy(
+            src_ref=relay.at[stage, v], dst_ref=lands[stage][k].at[v],
+            send_sem=pass_sem.at[stage], recv_sem=recv_sem.at[stage, k, v],
+            device_id=(ends[k][2], twin), device_id_type=mesh_id,
+        )
+
+    def forward(stage, v):
+        for k in range(2):
+
+            def hand_on(k=k):
+                detour(stage, k, v).wait_recv()
+                onward(stage, k, v).start()
+
+            pl.when((me_c == ends[k][1]) & relaying)(hand_on)
+
+    def forwarded(stage):
+        def wait():
+            pltpu.make_async_remote_copy(
+                src_ref=relay.at[stage], dst_ref=relay.at[stage],
+                send_sem=pass_sem.at[stage], recv_sem=relay_sem.at[stage, 0],
+                device_id=(me_c, twin), device_id_type=mesh_id,
+            ).wait_send()
+
+        pl.when(((me_c == ends[0][1]) | (me_c == ends[1][1])) & relaying)(wait)
+
     def launch(stage, axis, v):
         sign = 1.0 if stage == 0 else -1.0
         for k in (2 * axis, 2 * axis + 1):
-            guarded(reachable(ways[k][0]), lambda k=k: message(stage, k, v).start())
+            if axis == 1:
+                message(stage, k, v).start()
+                continue
+            indirect = (me_c == ends[k][0]) & detoured
+            direct = reachable(ways[k][0]) & jnp.logical_not(indirect)
+            pl.when(direct)(lambda k=k: message(stage, k, v).start())
+            pl.when(indirect)(lambda k=k: detour(stage, k, v).start())
         if axis == 0:
             for k in range(2):
 
@@ -342,7 +396,9 @@
     send_traces(1, 0)
     send_traces(0, 0)
     sides = jnp.where(me_c > 0, 1, 0) + jnp.where(me_c + 1 < chord_size, 1, 0)
-    pl.semaphore_wait(barrier, 2 + 3 * sides)
+    turns = jnp.where(relaying, jnp.where((me_c == ends[0][1]) | (me_c == ends[1][1]), 1, 0), 0)
+    turns += jnp.where(detoured, jnp.where((me_c == ends[0][0]) | (me_c == ends[1][0]), 1, 0), 0)
+    pl.semaphore_wait(barrier, 2 + 3 * sides + turns)
     for dx, dy in offsets:
         guarded(reachable(dx), lambda dx=dx, dy=dy: eps_copy(dx, dy).start())
     launch(0, 0, 0)
@@ -376,6 +432,8 @@
         return carry
 
     lax.fori_loop(0, count, normal_gradient, 0)
+    for v in range(3):
+        forward(0, v)
 
     row = lax.broadcasted_iota(jnp.int32, (rows, lanes), 0)
     for dx, dy in offsets:
@@ -404,6 +462,8 @@
         neighbours[1].append(inner)
         neighbours[2].append(jnp.where(closed_high, 0.0, above))
     interpolate(neighbours, nu)
+    for v in range(3, count):
+        forward(0, v)
 
     def flux(axis, v):
         low, high = masks[axis]
@@ -459,11 +519,15 @@
         lax.fori_loop(0, 5, body, 0, unroll=True)
         return carry
 
+    forward(1, 0)
     lax.fori_loop(0, count, normal, 0)
+    for v in range(1, 3):
+        forward(1, v)
 
     weight_c, weight_s = weights(0, masks), weights(1, masks)
 
     def correct(v, carry):
+        pl.when(v + 3 < count)(lambda: forward(1, v + 3))
         for axis in range(2):
             arrived(1, axis, v)
         for f in range(25):
@@ -484,6 +548,7 @@
     for stage in range(2):
         for k in range(4):
             guarded(reachable(ways[k][0]), lambda stage=stage, k=k: sent(stage, k).wait_send())
+        forwarded(stage)
 
 
 def shards(state):
@@ -516,6 +581,7 @@
                 (2, count, 50, rows, lanes),
                 (2, 25, rows, lanes),
                 (2, 25, rows, lanes),
+                (2, *message(count, 0)),
             ]
             + [message(count, k) for k in range(4)] * 4
         ]
@@ -525,6 +591,8 @@
             pltpu.SemaphoreType.DMA((9,)),
             pltpu.SemaphoreType.DMA((2, 4)),
             pltpu.SemaphoreType.DMA((2, 4, count)),
+            pltpu.SemaphoreType.DMA((2, count)),
+            pltpu.SemaphoreType.DMA((2,)),
         ],
         compiler_params=pltpu.CompilerParams(
             collective_id=0, has_side_effects=True, vmem_limit_bytes=VMEM_BYTES

time: 28.7 us -> 26.7 us (0.930)
  the two profiles are of different devices: /device:TPU:9 before, /device:TPU:99 now
where the time goes in v2:
time: 26.7 us; the launch traced here: 26.5 us
  Pallas kernels  23.6 us (88%)
  local copies, waits for them, and re-layouts  2.26 us (8%)
  between operations  0.64 us (2%)
    pallas_call x1, Pallas kernels, shards(): pl.pallas_call(functools.partial(local_kernel, sizes, count, chords, span...  23.6 us
    unnamed x2, local copies, waits for them, and re-layouts  2.26 us

profile of v2, /device:TPU:99, one launch (start us, length us, event | category | flops | bytes accessed | tf_op | source)
XLA Modules:
  0.0 26.5 jit_solution(1094776642179127200)
XLA Ops:
  0.6 23.6 %shard_map.30 = (f32[125,8,128]{2,1,0:T(8,128)S(1)}, f32[5,125,8,128]{3,2,1,0:T(8,128)S(1)}) custom-call(f32[5,125,8,128]{3,2,1,0:T(8,128)} %bitcast.5), custom_call_target="tpu_custom_call" | custom-call | tf_op jit(solution)/shard_map/pallas_call | solution.py:568
  24.3 1.5 %copy.5 = f32[5,125,4,2,128]{4,3,2,1,0:T(2,128)} copy(f32[5,125,4,2,128]{4,3,2,1,0:T(2,128)S(1)} %bitcast.3) | data formatting | bytes 5120000
  25.8 0.8 %copy.6 = f32[125,4,2,128]{3,2,1,0:T(2,128)} copy(f32[125,4,2,128]{3,2,1,0:T(2,128)S(1)} %bitcast.4) | data formatting | bytes 1024000

commit v3 on v1

--- a/solution.py
+++ b/solution.py
@@ -199,6 +199,7 @@
             edge = [lower[b] * face[0, z] + upper[b] * face[1, z] for z in range(2)]
             for c in range(5):
                 nu[25 * a + 5 * b + c] = lower[c] * edge[0] + upper[c] * edge[1]
+    return corner
 
 
 def row_masks(axis, chords, spans, lanes):
@@ -226,11 +227,10 @@
 def local_kernel(sizes, count, chords, spans, *refs):
     state_hbm = refs[0]
     nu, acc = refs[1:3]
-    state, grad, around, work, eps_out, faces, outside, lifted, t0, t1, t2, t3, f0, f1, f2, f3 = refs[3:19]
-    ghosts, flux_ghosts = refs[19:23], refs[23:27]
-    load_sem, eps_send, eps_recv, send_sem, recv_sem = refs[27:]
-    sends = ((t0, t1, t2, t3), (f0, f1, f2, f3))
-    lands = (ghosts, flux_ghosts)
+    state, grad, halo, work, faces, lifted, beta, spread, relay = refs[3:12]
+    sends = (refs[12:16], refs[16:20])
+    lands = (refs[20:24], refs[24:28])
+    load_sem, eps_send, eps_recv, send_sem, recv_sem, relay_sem, pass_sem = refs[28:]
     rows, lanes = nu.shape[1:]
     chord_size, span_size = sizes
     me_c, me_s = lax.axis_index("chord"), lax.axis_index("span")
@@ -250,7 +250,27 @@
     def partner(dx, dy):
         return (me_c + dx, lax.rem(me_s + dy + span_size, span_size))
 
+    cut, final = chord_size // 2, chord_size - 1
+    ends = ((cut - 1, cut), (cut, cut - 1))
+    twin = me_s + 1 - 2 * lax.rem(me_s, 2)
+    detoured = lax.rem((me_s + 1) // 2, 2) == 1
+    relaying = jnp.logical_not(detoured)
+    longer = 2
+    routes = (
+        ((0, True, 0, count - longer), (1, True, count - longer, count), (2, False, count - longer, count)),
+        ((0, True, longer, count), (1, True, 0, longer), (2, False, 0, longer)),
+    )
+
+    def place(k, depth):
+        return depth if k == 0 else final - depth
+
+    def mate(twinned):
+        return twin if twinned else me_s
+
     offsets = [(dx, dy) for dx in (0, -1, 1) for dy in (-1, 0, 1) if (dx, dy) != (0, 0)]
+    for r in range(chords + 4):
+        for q in range(spans + 4):
+            halo[r, q] = jnp.zeros((1, lanes), jnp.float32)
     barrier = pltpu.get_barrier_semaphore()
     for dx, dy in offsets:
 
@@ -259,16 +279,42 @@
 
         guarded(reachable(dx), greet)
 
+    extra = 0
+    for k, (source, target) in enumerate(ends):
+        for depth, twinned, _, _ in routes[0]:
+            through = place(k, depth)
+            sender = detoured if twinned else relaying
+            hops = [(target, sender, through, relaying)]
+            if twinned:
+                hops.append((through, relaying, source, sender))
+            for here, ready, there, awaiting in hops:
+
+                def greet_relay(there=there, twinned=twinned):
+                    pl.semaphore_signal(
+                        barrier, inc=1, device_id=(there, mate(twinned)), device_id_type=mesh_id
+                    )
+
+                pl.when((me_c == here) & ready)(greet_relay)
+                extra += jnp.where((me_c == there) & awaiting, 1, 0)
+
     def load(v):
         return pltpu.make_async_copy(state_hbm.at[v], state.at[v], load_sem.at[v])
 
     for v in range(count):
         load(v).start()
+
+    def layer(d, length, inside):
+        if d == 0:
+            return pl.ds(2, length)
+        if inside:
+            return pl.ds(length if d == 1 else 2, 2)
+        return pl.ds(0 if d == 1 else length + 2, 2)
 
     def eps_copy(dx, dy):
         slot = 3 * (dx + 1) + dy + 1
         return pltpu.make_async_remote_copy(
-            src_ref=eps_out, dst_ref=around.at[1 - dx, 1 - dy],
+            src_ref=halo.at[layer(dx, chords, True), layer(dy, spans, True)],
+            dst_ref=halo.at[layer(dx, chords, False), layer(dy, spans, False)],
             send_sem=eps_send.at[slot], recv_sem=eps_recv.at[8 - slot],
             device_id=partner(dx, dy), device_id_type=mesh_id,
         )
@@ -291,15 +337,76 @@
             device_id=partner(dx, dy), device_id_type=mesh_id,
         )
 
+    def detour(stage, k, v, route):
+        return pltpu.make_async_remote_copy(
+            src_ref=sends[stage][k].at[v], dst_ref=relay.at[stage, v],
+            send_sem=send_sem.at[stage, k], recv_sem=relay_sem.at[stage, v],
+            device_id=(place(k, route[0]), mate(route[1])), device_id_type=mesh_id,
+        )
+
+    def onward(stage, k, v, route):
+        return pltpu.make_async_remote_copy(
+            src_ref=relay.at[stage, v], dst_ref=lands[stage][k].at[v],
+            send_sem=pass_sem.at[stage, v], recv_sem=recv_sem.at[stage, k, v],
+            device_id=(ends[k][1], mate(route[1])), device_id_type=mesh_id,
+        )
+
+    posts = [place(k, route[0]) for k in range(2) for route in routes[0]]
+    on_post = functools.reduce(jnp.logical_or, [me_c == c for c in posts]) & relaying
+
+    def each_relay(stage, variables, run):
+        def roles():
+            for k in range(2):
+                for route in routes[stage]:
+
+                    def role(k=k, route=route):
+                        for v in variables:
+                            if route[2] <= v < route[3]:
+                                run(k, v, route)
+
+                    pl.when(me_c == place(k, route[0]))(role)
+
+        pl.when(on_post)(roles)
+
+    def forward(stage, variables):
+        def hand_on(k, v, route):
+            detour(stage, k, v, route).wait_recv()
+            onward(stage, k, v, route).start()
+
+        each_relay(stage, variables, hand_on)
+
+    def forwarded(stage):
+        each_relay(
+            stage, range(count), lambda k, v, route: onward(stage, k, v, route).wait_send()
+        )
+
     def launch(stage, axis, v):
-        sign = 1.0 if stage == 0 else -1.0
         for k in (2 * axis, 2 * axis + 1):
-            guarded(reachable(ways[k][0]), lambda k=k: message(stage, k, v).start())
+            if axis == 1:
+                message(stage, k, v).start()
+                continue
+            at_cut = me_c == ends[k][0]
+
+            def cross(k=k):
+                direct = me_c == ends[k][0]
+                for route in routes[stage]:
+                    takes = (detoured if route[1] else relaying) & (v >= route[2]) & (v < route[3])
+                    direct = direct & jnp.logical_not(takes)
+                    pl.when(takes)(lambda route=route: detour(stage, k, v, route).start())
+                pl.when(direct)(lambda: message(stage, k, v).start())
+
+            pl.when(at_cut)(cross)
+            pl.when(reachable(ways[k][0]) & jnp.logical_not(at_cut))(
+                lambda k=k: message(stage, k, v).start()
+            )
         if axis == 0:
             for k in range(2):
 
                 def mirror(k=k):
-                    lands[stage][1 - k][v] = sign * sends[stage][k][v]
+                    if stage == 0:
+                        lands[0][1 - k][v] = jnp.zeros(lands[0][1 - k].shape[1:], jnp.float32)
+                    else:
+                        lands[1][1 - k][v] = -sends[1][k][v]
 
                 pl.when(jnp.logical_not(reachable(ways[k][0])))(mirror)
 
@@ -333,16 +440,15 @@
 
         lax.fori_loop(0, 5, body, 0)
 
-    for f in range(25):
-        lifted[0, f] = jnp.zeros((rows, lanes), jnp.float32)
     load(0).wait()
     eps = sensor(lambda p: state[0, p], work)
-    eps_out[...] = eps
-    around[1, 1] = eps
+    lifted[1, 0] = eps
+    for r in range(rows):
+        halo[2 + r // spans, 2 + r % spans] = lifted[1, 0, pl.ds(r, 1)]
     send_traces(1, 0)
     send_traces(0, 0)
     sides = jnp.where(me_c > 0, 1, 0) + jnp.where(me_c + 1 < chord_size, 1, 0)
-    pl.semaphore_wait(barrier, 2 + 3 * sides)
+    pl.semaphore_wait(barrier, 2 + 3 * sides + extra)
     for dx, dy in offsets:
         guarded(reachable(dx), lambda dx=dx, dy=dy: eps_copy(dx, dy).start())
     launch(0, 0, 0)
@@ -360,108 +466,156 @@
     lane = lax.broadcasted_iota(jnp.int32, (rows, lanes), 1)
     first, last = lane == 0, lane == lanes - 1
 
-    def normal_gradient(v, carry):
-        def body(q, carry):
-            for j in range(5):
-                pts = points(2, q, j)
-                parts = fold([state[v, p] for p in pts])
-                left, right = traces(parts)
-                before = jnp.where(first, left, rolled(right, 1, 1))
-                after = jnp.where(last, right, rolled(left, -1, 1))
-                for p, value in zip(pts, slope(parts, before, after)):
-                    grad[v, p] = value
-            return carry
-
-        lax.fori_loop(0, 5, body, 0, unroll=True)
-        return carry
-
-    lax.fori_loop(0, count, normal_gradient, 0)
-
     row = lax.broadcasted_iota(jnp.int32, (rows, lanes), 0)
-    for dx, dy in offsets:
-        guarded(reachable(-dx), lambda dx=dx, dy=dy: eps_copy(dx, dy).wait_recv())
-
-    have_low = jnp.where(me_c > 0, spans, 0)
-    have_high = jnp.where(me_c + 1 < chord_size, rows, rows - spans)
-    low_s, high_s = masks[1]
-    low_c, high_c = masks[0]
-    column = []
-    for x in range(3):
-        mine, left, right = around[x, 1], around[x, 0], around[x, 2]
-        column.append([
-            jnp.where(low_s, rolled(left, 1 - spans, 0), rolled(mine, 1, 0)),
-            mine,
-            jnp.where(high_s, rolled(right, spans - 1, 0), rolled(mine, -1, 0)),
-        ])
-    closed_low = row < spans - have_low
-    closed_high = row >= have_high
-    neighbours = [[], [], []]
-    for y in range(3):
-        inner = column[1][y]
-        below = jnp.where(low_c, rolled(column[0][y], spans, 0), rolled(inner, spans, 0))
-        above = jnp.where(high_c, rolled(column[2][y], -spans, 0), rolled(inner, -spans, 0))
-        neighbours[0].append(jnp.where(closed_low, 0.0, below))
-        neighbours[1].append(inner)
-        neighbours[2].append(jnp.where(closed_high, 0.0, above))
-    interpolate(neighbours, nu)
-
-    def flux(axis, v):
+    closed_low = row < spans - jnp.where(me_c > 0, spans, 0)
+    closed_high = row >= jnp.where(me_c + 1 < chord_size, rows, rows - spans)
+
+    def inner(axis, left, right):
         low, high = masks[axis]
         step = spans if axis == 0 else 1
-
+        before = jnp.where(low, 0.0, rolled(right, step, 0))
+        return before, jnp.where(high, 0.0, rolled(left, -step, 0))
+
+    def local_gradients(v, carry):
         def body(q, carry):
             for j in range(5):
                 f = 5 * q + j
-                pts = points(axis, q, j)
-                parts = fold([state[v, p] for p in pts])
-                left, right = faces[axis, v, 2 * f], faces[axis, v, 2 * f + 1]
-                ghost = gather(0, axis, v, f, outside)
-                before = jnp.where(low, ghost, rolled(right, step, 0))
-                after = jnp.where(high, ghost, rolled(left, -step, 0))
-                gradient = slope(parts, before, after)
-                parts = fold([nu[p] * g for p, g in zip(pts, gradient)])
-                left, right = traces(parts)
+                for axis in range(3):
+                    pts = points(axis, q, j)
+                    parts = fold([state[v, p] for p in pts])
+                    if axis == 2:
+                        left, right = traces(parts)
+                        before = jnp.where(first, left, rolled(right, 1, 1))
+                        after = jnp.where(last, right, rolled(left, -1, 1))
+                    else:
+                        left, right = faces[axis, v, 2 * f], faces[axis, v, 2 * f + 1]
+                        before, after = inner(axis, left, right)
+                    if axis == 0:
+                        before = jnp.where(closed_low, left, before)
+                        after = jnp.where(closed_high, right, after)
+                    for p, value in zip(pts, slope(parts, before, after)):
+                        grad[axis, v, p] = value
+            return carry
+
+        lax.fori_loop(0, 5, body, 0, unroll=True)
+        return carry
+
+    lax.fori_loop(0, count, local_gradients, 0)
+
+    for dx, dy in offsets:
+        guarded(reachable(-dx), lambda dx=dx, dy=dy: eps_copy(dx, dy).wait_recv())
+    forward(0, range(count))
+
+    def shifted(x, y, slot):
+        for r in range(rows):
+            lifted[1, slot, pl.ds(r, 1)] = halo[2 + x + r // spans, 2 + y + r % spans]
+        return lifted[1, slot]
+
+    near = {(x, y): shifted(x, y, 3 * x + y + 4) for x in (-1, 0, 1) for y in (-1, 0, 1)}
+    neighbours = [[near[x, y] for y in (-1, 0, 1)] for x in (-1, 0, 1)]
+    corner = interpolate(neighbours, nu)
+    near_weight = sum(float(LEFT[i] * HALF_LEFT[i] * (1.0 - NODES[i]) / 2.0) for i in range(5))
+    far_weight = sum(float(LEFT[i] * HALF_LEFT[i] * (1.0 + NODES[i]) / 2.0) for i in range(5))
+    slot = 9
+    for axis in range(2):
+        low = masks[axis][0]
+        sign = jnp.where(low, -1.0, 1.0)
+        lines = []
+        for t in (-1, 0, 1):
+            beyond = []
+            for d in (-2, 2):
+                x, y = (d, t) if axis == 0 else (t, d)
+                beyond.append(shifted(x, y, slot))
+                slot += 1
+            close = [near[d, t] if axis == 0 else near[t, d] for d in (-1, 1)]
+            lines.append(jnp.maximum(jnp.where(low, *beyond), jnp.where(low, *close)))
+        weight = {}
+        for t in range(2):
+            far = along_lanes(jnp.maximum(lines[t], lines[t + 1]))
+            for z in range(2):
+                if axis == 0:
+                    shared = jnp.where(low, corner[0, t, z], corner[1, t, z])
+                else:
+                    shared = jnp.where(low, corner[t, 0, z], corner[t, 1, z])
+                value = sign * (near_weight * shared + far_weight * far[z])
+                if axis == 0:
+                    value = jnp.where(closed_low | closed_high, 0.0, value)
+                weight[t, z] = value
+        for m in range(5):
+            edge = [LOWER[m] * weight[0, z] + UPPER[m] * weight[1, z] for z in range(2)]
+            for c in range(5):
+                beta[axis, 5 * m + c] = LOWER[c] * edge[0] + UPPER[c] * edge[1]
+
+    def flux(axis, v):
+        def body(q, carry):
+            for j in range(5):
+                f = 5 * q + j
+                values = []
+                for p in points(axis, q, j):
+                    values.append(nu[p] * grad[axis, v, p])
+                    grad[axis, v, p] = values[-1]
+                left, right = traces(fold(values))
                 work[2 * f] = left
                 work[2 * f + 1] = right
                 extract(1, axis, v, f, work, (2 * f,))
-                before = jnp.where(low, 0.0, rolled(right, step, 0))
-                after = jnp.where(high, 0.0, rolled(left, -step, 0))
-                for p, value in zip(pts, slope(parts, before, after)):
-                    if axis == 0:
-                        acc[v, p] = value
-                    else:
-                        acc[v, p] += value
             return carry
 
         lax.fori_loop(0, 5, body, 0, unroll=True)
 
-    def variable(v, carry):
+    def fluxes(v, carry):
         for axis in range(2):
-            arrived(0, axis, v)
             flux(axis, v)
             launch(1, axis, v)
         return carry
 
-    lax.fori_loop(0, count, variable, 0)
-
+    lax.fori_loop(0, count, fluxes, 0)
     def normal(v, carry):
         def body(q, carry):
             for j in range(5):
                 pts = points(2, q, j)
-                parts = fold([nu[p] * grad[v, p] for p in pts])
+                parts = fold([nu[p] * grad[2, v, p] for p in pts])
                 left, right = traces(parts)
                 before = jnp.where(first, -left, rolled(right, 1, 1))
                 after = jnp.where(last, -right, rolled(left, -1, 1))
                 for p, value in zip(pts, slope(parts, before, after)):
-                    acc[v, p] += value
+                    acc[v, p] = value
             return carry
 
         lax.fori_loop(0, 5, body, 0, unroll=True)
         return carry
 
     lax.fori_loop(0, count, normal, 0)
-
-    weight_c, weight_s = weights(0, masks), weights(1, masks)
+    forward(1, range(longer))
+
+    lift = [weights(axis, masks) for axis in range(2)]
+    for f in range(25):
+        lifted[0, f] = jnp.zeros((rows, lanes), jnp.float32)
+        for axis in range(2):
+            for p, w in zip(points(axis, f // 5, f % 5), lift[axis]):
+                spread[axis, p] = nu[p] * w
+
+    def divergence(v, carry):
+        for axis in range(2):
+            arrived(0, axis, v)
+
+        def body(q, carry):
+            for j in range(5):
+                f = 5 * q + j
+                for axis in range(2):
+                    pts = points(axis, q, j)
+                    ghost = gather(0, axis, v, f, lifted)
+                    parts = fold([grad[axis, v, p] + spread[axis, p] * ghost for p in pts])
+                    before, after = inner(axis, *traces(parts))
+                    for p, value in zip(pts, slope(parts, before, after)):
+                        acc[v, p] += value
+            return carry
+
+        lax.fori_loop(0, 5, body, 0, unroll=True)
+        for w in range(longer, count):
+            pl.when(v == w - 1)(lambda w=w: forward(1, (w,)))
+        return carry
+
+    lax.fori_loop(0, count, divergence, 0)
 
     def correct(v, carry):
         for axis in range(2):
@@ -469,12 +623,17 @@
         for f in range(25):
             for axis in range(2):
                 gather(1, axis, v, f, lifted)
+
+        def outer_flux(axis, f):
+            own = jnp.where(masks[axis][0], faces[axis, v, 2 * f], faces[axis, v, 2 * f + 1])
+            return lifted[axis, f] + beta[axis, f] * own
+
         for c in range(5):
-            across = [lifted[0, 5 * b + c] for b in range(5)]
+            across = [outer_flux(0, 5 * b + c) for b in range(5)]
             for a in range(5):
-                along = lifted[1, 5 * a + c]
+                along = outer_flux(1, 5 * a + c)
                 for b in range(5):
-                    acc[v, 25 * a + 5 * b + c] += weight_c[a] * across[b] + weight_s[b] * along
+                    acc[v, 25 * a + 5 * b + c] += lift[0][a] * across[b] + lift[1][b] * along
         return carry
 
     lax.fori_loop(0, count, correct, 0)
@@ -484,6 +643,7 @@
     for stage in range(2):
         for k in range(4):
             guarded(reachable(ways[k][0]), lambda stage=stage, k=k: sent(stage, k).wait_send())
+        forwarded(stage)
 
 
 def shards(state):
@@ -509,13 +669,14 @@
             pltpu.VMEM(shape, f32)
             for shape in [
                 (count, npts, rows, lanes),
-                (count, npts, rows, lanes),
-                (3, 3, rows, lanes),
+                (3, count, npts, rows, lanes),
+                (chords + 4, spans + 4, 1, lanes),
                 (npts, rows, lanes),
-                (rows, lanes),
                 (2, count, 50, rows, lanes),
                 (2, 25, rows, lanes),
                 (2, 25, rows, lanes),
+                (2, npts, rows, lanes),
+                (2, *message(count, 0)),
             ]
             + [message(count, k) for k in range(4)] * 4
         ]
@@ -525,6 +686,8 @@
             pltpu.SemaphoreType.DMA((9,)),
             pltpu.SemaphoreType.DMA((2, 4)),
             pltpu.SemaphoreType.DMA((2, 4, count)),
+            pltpu.SemaphoreType.DMA((2, count)),
+            pltpu.SemaphoreType.DMA((2, count)),
         ],
         compiler_params=pltpu.CompilerParams(
             collective_id=0, has_side_effects=True, vmem_limit_bytes=VMEM_BYTES

time: 28.7 us -> 25.8 us (0.90)
  the two profiles are of different devices: /device:TPU:9 before, /device:TPU:8 now
where the time goes in v3:
time: 25.8 us; the launch traced here: 25.7 us
  Pallas kernels  22.8 us (88%)
  local copies, waits for them, and re-layouts  2.26 us (9%)
  between operations  0.64 us (2%)
    pallas_call x1, Pallas kernels, shards(): pl.pallas_call(functools.partial(local_kernel, sizes, count, chords, span...  22.8 us
    unnamed x2, local copies, waits for them, and re-layouts  2.26 us

profile of v3, /device:TPU:8, one launch (start us, length us, event | category | flops | bytes accessed | tf_op | source)
XLA Modules:
  0.0 25.7 jit_solution(11740701204989084303)
XLA Ops:
  0.6 22.8 %shard_map.30 = (f32[125,8,128]{2,1,0:T(8,128)S(1)}, f32[5,125,8,128]{3,2,1,0:T(8,128)S(1)}) custom-call(f32[5,125,8,128]{3,2,1,0:T(8,128)} %bitcast.5), custom_call_target="tpu_custom_call" | custom-call | tf_op jit(solution)/shard_map/pallas_call | solution.py:663
  23.4 1.5 %copy.5 = f32[5,125,4,2,128]{4,3,2,1,0:T(2,128)} copy(f32[5,125,4,2,128]{4,3,2,1,0:T(2,128)S(1)} %bitcast.3) | data formatting | bytes 5120000
  24.9 0.8 %copy.6 = f32[125,4,2,128]{3,2,1,0:T(2,128)} copy(f32[125,4,2,128]{3,2,1,0:T(2,128)S(1)} %bitcast.4) | data formatting | bytes 1024000

commit v4 on v3

--- a/solution.py
+++ b/solution.py
@@ -257,8 +257,8 @@
     relaying = jnp.logical_not(detoured)
     longer = 2
     routes = (
-        ((0, True, 0, count - longer), (1, True, count - longer, count), (2, False, count - longer, count)),
-        ((0, True, longer, count), (1, True, 0, longer), (2, False, 0, longer)),
+        ((0, True, 0, longer), (1, True, longer, count), (2, False, longer, count)),
+        ((0, True, 0, count),),
     )
 
     def place(k, depth):
@@ -504,7 +504,7 @@
 
     for dx, dy in offsets:
         guarded(reachable(-dx), lambda dx=dx, dy=dy: eps_copy(dx, dy).wait_recv())
-    forward(0, range(count))
+    forward(0, range(3))
 
     def shifted(x, y, slot):
         for r in range(rows):
@@ -569,6 +569,7 @@
         return carry
 
     lax.fori_loop(0, count, fluxes, 0)
+    forward(0, range(3, count))
     def normal(v, carry):
         def body(q, carry):
             for j in range(5):
@@ -585,7 +586,7 @@
         return carry
 
     lax.fori_loop(0, count, normal, 0)
-    forward(1, range(longer))
+    forward(1, range(2))
 
     lift = [weights(axis, masks) for axis in range(2)]
     for f in range(25):
@@ -611,7 +612,7 @@
             return carry
 
         lax.fori_loop(0, 5, body, 0, unroll=True)
-        for w in range(longer, count):
+        for w in range(2, count):
             pl.when(v == w - 1)(lambda w=w: forward(1, (w,)))
         return carry
 
@@ -644,6 +645,18 @@
         for k in range(4):
             guarded(reachable(ways[k][0]), lambda stage=stage, k=k: sent(stage, k).wait_send())
         forwarded(stage)
+
+
+def write_kernel(nu, residual, nu_hbm, residual_hbm, sems):
+    copies = [
+        pltpu.make_async_copy(residual.at[v], residual_hbm.at[v], sems.at[v])
+        for v in range(residual.shape[0])
+    ]
+    copies.append(pltpu.make_async_copy(nu, nu_hbm, sems.at[residual.shape[0]]))
+    for copy in copies:
+        copy.start()
+    for copy in copies:
+        copy.wait()
 
 
 def shards(state):
@@ -693,6 +706,15 @@
             collective_id=0, has_side_effects=True, vmem_limit_bytes=VMEM_BYTES
         ),
     )(flat)
+    hbm = pl.BlockSpec(memory_space=pltpu.HBM)
+    nu, residual = pl.pallas_call(
+        write_kernel,
+        in_specs=[vmem, vmem],
+        out_specs=[hbm, hbm],
+        out_shape=[full(npts, rows, lanes), full(count, npts, rows, lanes)],
+        scratch_shapes=[pltpu.SemaphoreType.DMA((count + 1,))],
+        compiler_params=pltpu.CompilerParams(vmem_limit_bytes=1_000_000),
+    )(nu, residual)
     return residual.reshape(state.shape), nu.reshape(npts, chords, spans, lanes)
 
 

time: 25.8 us -> 24.6 us (0.953)
  the two profiles are of different devices: /device:TPU:8 before, /device:TPU:9 now
where the time goes in v4:
time: 24.6 us; the launch traced here: 24.4 us
  Pallas kernels  23.8 us (97%)
  between operations  0.64 us (3%)
    pallas_call x1, Pallas kernels, shards(): pl.pallas_call(functools.partial(local_kernel, sizes, count, chords, span...  22.1 us
    pallas_call x1, Pallas kernels, shards(): pl.pallas_call(write_kernel, in_specs=[vmem, vmem], out_specs=[hbm, hbm],...  1.68 us

profile of v4, /device:TPU:9, one launch (start us, length us, event | category | flops | bytes accessed | tf_op | source)
XLA Modules:
  0.0 24.4 jit_solution(1150005028538921151)
XLA Ops:
  0.6 22.1 %shard_map.30 = (f32[125,8,128]{2,1,0:T(8,128)S(1)}, f32[5,125,8,128]{3,2,1,0:T(8,128)S(1)}) custom-call(f32[5,125,8,128]{3,2,1,0:T(8,128)} %bitcast.3), custom_call_target="tpu_custom_call" | custom-call | tf_op jit(solution)/shard_map/pallas_call | solution.py:676
  22.8 1.7 %shard_map.31 = (f32[125,8,128]{2,1,0:T(8,128)}, f32[5,125,8,128]{3,2,1,0:T(8,128)}) custom-call(f32[125,8,128]{2,1,0:T(8,128)S(1)} %get-tuple-element.6.nu, f32[5,125,8,128]{3,2,1,0:T(8,128)S(1)} %get-tuple-element.7.residual), custom_call_target="tpu_custom_call" | custom-call | tf_op jit(solution)/shard_map/pallas_call | solution.py:710

commit v5 on v4

--- a/solution.py
+++ b/solution.py
@@ -256,10 +256,11 @@
     detoured = lax.rem((me_s + 1) // 2, 2) == 1
     relaying = jnp.logical_not(detoured)
     longer = 2
-    routes = (
-        ((0, True, 0, longer), (1, True, longer, count), (2, False, longer, count)),
-        ((0, True, 0, count),),
+    ghost_routes = (
+        (0, True, 0, longer, 0), (1, True, longer, count, 0), (2, False, longer, count, 0),
     )
+    near, shifted_from = (0, True, 0, count, 1), 1
+    routes = ((ghost_routes, ghost_routes), ((near,), (near, (0, False, shifted_from, count, 2))))
 
     def place(k, depth):
         return depth if k == 0 else final - depth
@@ -281,11 +282,11 @@
 
     extra = 0
     for k, (source, target) in enumerate(ends):
-        for depth, twinned, _, _ in routes[0]:
+        for depth, twinned in sorted({r[:2] for stage in routes for r in stage[k]}):
             through = place(k, depth)
             sender = detoured if twinned else relaying
             hops = [(target, sender, through, relaying)]
-            if twinned:
+            if twinned or abs(through - source) > 1:
                 hops.append((through, relaying, source, sender))
             for here, ready, there, awaiting in hops:
 
@@ -339,25 +340,25 @@
 
     def detour(stage, k, v, route):
         return pltpu.make_async_remote_copy(
-            src_ref=sends[stage][k].at[v], dst_ref=relay.at[stage, v],
-            send_sem=send_sem.at[stage, k], recv_sem=relay_sem.at[stage, v],
+            src_ref=sends[stage][k].at[v], dst_ref=relay.at[route[4], v],
+            send_sem=send_sem.at[stage, k], recv_sem=relay_sem.at[route[4], v],
             device_id=(place(k, route[0]), mate(route[1])), device_id_type=mesh_id,
         )
 
     def onward(stage, k, v, route):
         return pltpu.make_async_remote_copy(
-            src_ref=relay.at[stage, v], dst_ref=lands[stage][k].at[v],
-            send_sem=pass_sem.at[stage, v], recv_sem=recv_sem.at[stage, k, v],
+            src_ref=relay.at[route[4], v], dst_ref=lands[stage][k].at[v],
+            send_sem=pass_sem.at[route[4], v], recv_sem=recv_sem.at[stage, k, v],
             device_id=(ends[k][1], mate(route[1])), device_id_type=mesh_id,
         )
 
-    posts = [place(k, route[0]) for k in range(2) for route in routes[0]]
+    posts = [place(k, route[0]) for k in range(2) for route in ghost_routes]
     on_post = functools.reduce(jnp.logical_or, [me_c == c for c in posts]) & relaying
 
     def each_relay(stage, variables, run):
         def roles():
             for k in range(2):
-                for route in routes[stage]:
+                for route in routes[stage][k]:
 
                     def role(k=k, route=route):
                         for v in variables:
@@ -389,7 +390,7 @@
 
             def cross(k=k):
                 direct = me_c == ends[k][0]
-                for route in routes[stage]:
+                for route in routes[stage][k]:
                     takes = (detoured if route[1] else relaying) & (v >= route[2]) & (v < route[3])
                     direct = direct & jnp.logical_not(takes)
                     pl.when(takes)(lambda route=route: detour(stage, k, v, route).start())
@@ -514,6 +515,31 @@
     near = {(x, y): shifted(x, y, 3 * x + y + 4) for x in (-1, 0, 1) for y in (-1, 0, 1)}
     neighbours = [[near[x, y] for y in (-1, 0, 1)] for x in (-1, 0, 1)]
     corner = interpolate(neighbours, nu)
+    def flux(axis, v):
+        def body(q, carry):
+            for j in range(5):
+                f = 5 * q + j
+                values = []
+                for p in points(axis, q, j):
+                    values.append(nu[p] * grad[axis, v, p])
+                    grad[axis, v, p] = values[-1]
+                left, right = traces(fold(values))
+                work[2 * f] = left
+                work[2 * f + 1] = right
+                extract(1, axis, v, f, work, (2 * f,))
+            return carry
+
+        lax.fori_loop(0, 5, body, 0, unroll=True)
+
+    def fluxes(v, carry):
+        for axis in range(2):
+            flux(axis, v)
+            launch(1, axis, v)
+        return carry
+
+    lax.fori_loop(0, count, fluxes, 0)
+    forward(0, range(3, count))
+
     near_weight = sum(float(LEFT[i] * HALF_LEFT[i] * (1.0 - NODES[i]) / 2.0) for i in range(5))
     far_weight = sum(float(LEFT[i] * HALF_LEFT[i] * (1.0 + NODES[i]) / 2.0) for i in range(5))
     slot = 9
@@ -545,31 +571,6 @@
             edge = [LOWER[m] * weight[0, z] + UPPER[m] * weight[1, z] for z in range(2)]
             for c in range(5):
                 beta[axis, 5 * m + c] = LOWER[c] * edge[0] + UPPER[c] * edge[1]
-
-    def flux(axis, v):
-        def body(q, carry):
-            for j in range(5):
-                f = 5 * q + j
-                values = []
-                for p in points(axis, q, j):
-                    values.append(nu[p] * grad[axis, v, p])
-                    grad[axis, v, p] = values[-1]
-                left, right = traces(fold(values))
-                work[2 * f] = left
-                work[2 * f + 1] = right
-                extract(1, axis, v, f, work, (2 * f,))
-            return carry
-
-        lax.fori_loop(0, 5, body, 0, unroll=True)
-
-    def fluxes(v, carry):
-        for axis in range(2):
-            flux(axis, v)
-            launch(1, axis, v)
-        return carry
-
-    lax.fori_loop(0, count, fluxes, 0)
-    forward(0, range(3, count))
     def normal(v, carry):
         def body(q, carry):
             for j in range(5):
@@ -586,7 +587,6 @@
         return carry
 
     lax.fori_loop(0, count, normal, 0)
-    forward(1, range(2))
 
     lift = [weights(axis, masks) for axis in range(2)]
     for f in range(25):
@@ -612,8 +612,7 @@
             return carry
 
         lax.fori_loop(0, 5, body, 0, unroll=True)
-        for w in range(2, count):
-            pl.when(v == w - 1)(lambda w=w: forward(1, (w,)))
+        pl.when(v == count - 2)(lambda: forward(1, range(count)))
         return carry
 
     lax.fori_loop(0, count, divergence, 0)
@@ -689,7 +688,7 @@
                 (2, 25, rows, lanes),
                 (2, 25, rows, lanes),
                 (2, npts, rows, lanes),
-                (2, *message(count, 0)),
+                (3, *message(count, 0)),
             ]
             + [message(count, k) for k in range(4)] * 4
         ]
@@ -699,8 +698,8 @@
             pltpu.SemaphoreType.DMA((9,)),
             pltpu.SemaphoreType.DMA((2, 4)),
             pltpu.SemaphoreType.DMA((2, 4, count)),
-            pltpu.SemaphoreType.DMA((2, count)),
-            pltpu.SemaphoreType.DMA((2, count)),
+            pltpu.SemaphoreType.DMA((3, count)),
+            pltpu.SemaphoreType.DMA((3, count)),
         ],
         compiler_params=pltpu.CompilerParams(
             collective_id=0, has_side_effects=True, vmem_limit_bytes=VMEM_BYTES

time: 24.6 us -> 23.8 us (0.967)
  Pallas kernels: 23.8 us -> 23 us
    pallas_call x1, Pallas kernels: 22.1 us -> 21.3 us  [shards(): pl.pallas_call(functools.partial(local_kernel, sizes, count, chords, span...]
where the time goes in v5:
time: 23.8 us; the launch traced here: 23.6 us
  Pallas kernels  23 us (97%)
  between operations  0.64 us (3%)
    pallas_call x1, Pallas kernels, shards(): pl.pallas_call(functools.partial(local_kernel, sizes, count, chords, span...  21.3 us
    pallas_call x1, Pallas kernels, shards(): pl.pallas_call(write_kernel, in_specs=[vmem, vmem], out_specs=[hbm, hbm],...  1.68 us

profile of v5, /device:TPU:9, one launch (start us, length us, event | category | flops | bytes accessed | tf_op | source)
XLA Modules:
  0.0 23.6 jit_solution(9843293555499321796)
XLA Ops:
  0.6 21.3 %shard_map.30 = (f32[125,8,128]{2,1,0:T(8,128)S(1)}, f32[5,125,8,128]{3,2,1,0:T(8,128)S(1)}) custom-call(f32[5,125,8,128]{3,2,1,0:T(8,128)} %bitcast.3), custom_call_target="tpu_custom_call" | custom-call | tf_op jit(solution)/shard_map/pallas_call | solution.py:675
  21.9 1.7 %shard_map.31 = (f32[125,8,128]{2,1,0:T(8,128)}, f32[5,125,8,128]{3,2,1,0:T(8,128)}) custom-call(f32[125,8,128]{2,1,0:T(8,128)S(1)} %get-tuple-element.6.nu, f32[5,125,8,128]{3,2,1,0:T(8,128)S(1)} %get-tuple-element.7.residual), custom_call_target="tpu_custom_call" | custom-call | tf_op jit(solution)/shard_map/pallas_call | solution.py:709

commit v6 on v5

--- a/solution.py
+++ b/solution.py
@@ -259,8 +259,9 @@
     ghost_routes = (
         (0, True, 0, longer, 0), (1, True, longer, count, 0), (2, False, longer, count, 0),
     )
-    near, shifted_from = (0, True, 0, count, 1), 1
-    routes = ((ghost_routes, ghost_routes), ((near,), (near, (0, False, shifted_from, count, 2))))
+    near, shifted_from = (0, True, 0, count, 1), 0
+    fore_routes = ((0, True, 0, 1, 0), (1, True, 1, count, 0), (2, False, longer, count, 0))
+    routes = ((fore_routes, ghost_routes), ((near,), (near, (0, False, shifted_from, count, 2))))
 
     def place(k, depth):
         return depth if k == 0 else final - depth
@@ -269,9 +270,10 @@
         return twin if twinned else me_s
 
     offsets = [(dx, dy) for dx in (0, -1, 1) for dy in (-1, 0, 1) if (dx, dy) != (0, 0)]
-    for r in range(chords + 4):
-        for q in range(spans + 4):
-            halo[r, q] = jnp.zeros((1, lanes), jnp.float32)
+    def load(v):
+        return pltpu.make_async_copy(state_hbm.at[v], state.at[v], load_sem.at[v])
+
+    load(0).start()
     barrier = pltpu.get_barrier_semaphore()
     for dx, dy in offsets:
 
@@ -298,11 +300,17 @@
                 pl.when((me_c == here) & ready)(greet_relay)
                 extra += jnp.where((me_c == there) & awaiting, 1, 0)
 
-    def load(v):
-        return pltpu.make_async_copy(state_hbm.at[v], state.at[v], load_sem.at[v])
-
-    for v in range(count):
+    for v in range(1, count):
         load(v).start()
+
+    for dx, rows_out in ((-1, (0, 1)), (1, (chords + 2, chords + 3))):
+
+        def close(rows_out=rows_out):
+            for r in rows_out:
+                for q in range(spans + 4):
+                    halo[r, q] = jnp.zeros((1, lanes), jnp.float32)
+
+        pl.when(jnp.logical_not(reachable(dx)))(close)
 
     def layer(d, length, inside):
         if d == 0:

time: 23.8 us -> 23.6 us (level)
  no operation moved by 1% of the time
where the time goes in v6:
time: 23.6 us; the launch traced here: 23.5 us
  Pallas kernels  22.8 us (97%)
  between operations  0.64 us (3%)
    pallas_call x1, Pallas kernels, shards(): pl.pallas_call(functools.partial(local_kernel, sizes, count, chords, span...  21.2 us
    pallas_call x1, Pallas kernels, shards(): pl.pallas_call(write_kernel, in_specs=[vmem, vmem], out_specs=[hbm, hbm],...  1.68 us

profile of v6, /device:TPU:9, one launch (start us, length us, event | category | flops | bytes accessed | tf_op | source)
XLA Modules:
  0.0 23.5 jit_solution(16920170773968443374)
XLA Ops:
  0.6 21.2 %shard_map.30 = (f32[125,8,128]{2,1,0:T(8,128)S(1)}, f32[5,125,8,128]{3,2,1,0:T(8,128)S(1)}) custom-call(f32[5,125,8,128]{3,2,1,0:T(8,128)} %bitcast.3), custom_call_target="tpu_custom_call" | custom-call | tf_op jit(solution)/shard_map/pallas_call | solution.py:683
  21.8 1.7 %shard_map.31 = (f32[125,8,128]{2,1,0:T(8,128)}, f32[5,125,8,128]{3,2,1,0:T(8,128)}) custom-call(f32[125,8,128]{2,1,0:T(8,128)S(1)} %get-tuple-element.6.nu, f32[5,125,8,128]{3,2,1,0:T(8,128)S(1)} %get-tuple-element.7.residual), custom_call_target="tpu_custom_call" | custom-call | tf_op jit(solution)/shard_map/pallas_call | solution.py:717

commit v7 on v6

--- a/solution.py
+++ b/solution.py
@@ -320,12 +320,18 @@
         return pl.ds(0 if d == 1 else length + 2, 2)
 
     def eps_copy(dx, dy):
-        slot = 3 * (dx + 1) + dy + 1
         return pltpu.make_async_remote_copy(
             src_ref=halo.at[layer(dx, chords, True), layer(dy, spans, True)],
             dst_ref=halo.at[layer(dx, chords, False), layer(dy, spans, False)],
-            send_sem=eps_send.at[slot], recv_sem=eps_recv.at[8 - slot],
+            send_sem=eps_send.at[dx + 1], recv_sem=eps_recv.at[1 - dx],
             device_id=partner(dx, dy), device_id_type=mesh_id,
+        )
+
+    def eps_group(dx):
+        part = halo.at[pl.ds(0, chords), pl.ds(0, 4)] if dx == 0 else halo.at[pl.ds(0, 2)]
+        return pltpu.make_async_remote_copy(
+            src_ref=part, dst_ref=part, send_sem=eps_send.at[dx + 1], recv_sem=eps_recv.at[dx + 1],
+            device_id=partner(dx, 1), device_id_type=mesh_id,
         )
 
     ways = ((1, 0), (-1, 0), (0, 1), (0, -1))
@@ -511,8 +517,8 @@
 
     lax.fori_loop(0, count, local_gradients, 0)
 
-    for dx, dy in offsets:
-        guarded(reachable(-dx), lambda dx=dx, dy=dy: eps_copy(dx, dy).wait_recv())
+    for dx in (0, -1, 1):
+        guarded(reachable(dx), lambda dx=dx: eps_group(dx).wait_recv())
     forward(0, range(3))
 
     def shifted(x, y, slot):
@@ -603,27 +609,28 @@
             for p, w in zip(points(axis, f // 5, f % 5), lift[axis]):
                 spread[axis, p] = nu[p] * w
 
-    def divergence(v, carry):
-        for axis in range(2):
+    for axis in (1, 0):
+
+        def divergence(v, carry):
             arrived(0, axis, v)
 
-        def body(q, carry):
-            for j in range(5):
-                f = 5 * q + j
-                for axis in range(2):
+            def body(q, carry):
+                for j in range(5):
+                    f = 5 * q + j
                     pts = points(axis, q, j)
                     ghost = gather(0, axis, v, f, lifted)
                     parts = fold([grad[axis, v, p] + spread[axis, p] * ghost for p in pts])
                     before, after = inner(axis, *traces(parts))
                     for p, value in zip(pts, slope(parts, before, after)):
                         acc[v, p] += value
+                return carry
+
+            lax.fori_loop(0, 5, body, 0, unroll=True)
+            if axis == 0:
+                pl.when(v == count - 3)(lambda: forward(1, range(count)))
             return carry
 
-        lax.fori_loop(0, 5, body, 0, unroll=True)
-        pl.when(v == count - 2)(lambda: forward(1, range(count)))
-        return carry
-
-    lax.fori_loop(0, count, divergence, 0)
+        lax.fori_loop(0, count, divergence, 0)
 
     def correct(v, carry):
         for axis in range(2):
@@ -646,8 +653,8 @@
 
     lax.fori_loop(0, count, correct, 0)
 
-    for dx, dy in offsets:
-        guarded(reachable(dx), lambda dx=dx, dy=dy: eps_copy(dx, dy).wait_send())
+    for dx in (0, -1, 1):
+        guarded(reachable(dx), lambda dx=dx: eps_group(dx).wait_send())
     for stage in range(2):
         for k in range(4):
             guarded(reachable(ways[k][0]), lambda stage=stage, k=k: sent(stage, k).wait_send())
@@ -702,8 +709,8 @@
         ]
         + [
             pltpu.SemaphoreType.DMA((count,)),
-            pltpu.SemaphoreType.DMA((9,)),
-            pltpu.SemaphoreType.DMA((9,)),
+            pltpu.SemaphoreType.DMA((3,)),
+            pltpu.SemaphoreType.DMA((3,)),
             pltpu.SemaphoreType.DMA((2, 4)),
             pltpu.SemaphoreType.DMA((2, 4, count)),
             pltpu.SemaphoreType.DMA((3, count)),

time: 23.6 us -> 23.5 us (level)
  no operation moved by 1% of the time
where the time goes in v7:
time: 23.5 us; the launch traced here: 23.4 us
  Pallas kernels  22.7 us (97%)
  between operations  0.64 us (3%)
    pallas_call x1, Pallas kernels, shards(): pl.pallas_call(functools.partial(local_kernel, sizes, count, chords, span...  21 us
    pallas_call x1, Pallas kernels, shards(): pl.pallas_call(write_kernel, in_specs=[vmem, vmem], out_specs=[hbm, hbm],...  1.68 us

profile of v7, /device:TPU:9, one launch (start us, length us, event | category | flops | bytes accessed | tf_op | source)
XLA Modules:
  0.0 23.4 jit_solution(2151178146063585881)
XLA Ops:
  0.6 21.0 %shard_map.30 = (f32[125,8,128]{2,1,0:T(8,128)S(1)}, f32[5,125,8,128]{3,2,1,0:T(8,128)S(1)}) custom-call(f32[5,125,8,128]{3,2,1,0:T(8,128)} %bitcast.3), custom_call_target="tpu_custom_call" | custom-call | tf_op jit(solution)/shard_map/pallas_call | solution.py:690
  21.7 1.7 %shard_map.31 = (f32[125,8,128]{2,1,0:T(8,128)}, f32[5,125,8,128]{3,2,1,0:T(8,128)}) custom-call(f32[125,8,128]{2,1,0:T(8,128)S(1)} %get-tuple-element.6.nu, f32[5,125,8,128]{3,2,1,0:T(8,128)S(1)} %get-tuple-element.7.residual), custom_call_target="tpu_custom_call" | custom-call | tf_op jit(solution)/shard_map/pallas_call | solution.py:724

commit v8 on v7

--- a/solution.py
+++ b/solution.py
@@ -340,7 +340,7 @@
         dx, dy = ways[k]
         return pltpu.make_async_remote_copy(
             src_ref=sends[stage][k].at[v], dst_ref=lands[stage][k].at[v],
-            send_sem=send_sem.at[stage, k], recv_sem=recv_sem.at[stage, k, v],
+            send_sem=send_sem.at[stage, k], recv_sem=recv_sem.at[stage, min(k, 2), v],
             device_id=partner(dx, dy), device_id_type=mesh_id,
         )
 
@@ -426,7 +426,15 @@
                 pl.when(jnp.logical_not(reachable(ways[k][0])))(mirror)
 
     def arrived(stage, axis, v):
-        for k in (2 * axis, 2 * axis + 1):
+        if axis == 1:
+            both = sends[stage][2].at[pl.ds(0, 2)]
+            pltpu.make_async_remote_copy(
+                src_ref=both, dst_ref=both, send_sem=send_sem.at[stage, 2],
+                recv_sem=recv_sem.at[stage, 2, v],
+                device_id=partner(0, 1), device_id_type=mesh_id,
+            ).wait_recv()
+            return
+        for k in range(2):
             guarded(reachable(-ways[k][0]), lambda k=k: message(stage, k, v).wait_recv())
 
     masks = [row_masks(axis, chords, spans, lanes) for axis in range(2)]
@@ -546,7 +554,7 @@
         lax.fori_loop(0, 5, body, 0, unroll=True)
 
     def fluxes(v, carry):
-        for axis in range(2):
+        for axis in (1, 0):
             flux(axis, v)
             launch(1, axis, v)
         return carry
@@ -712,7 +720,7 @@
             pltpu.SemaphoreType.DMA((3,)),
             pltpu.SemaphoreType.DMA((3,)),
             pltpu.SemaphoreType.DMA((2, 4)),
-            pltpu.SemaphoreType.DMA((2, 4, count)),
+            pltpu.SemaphoreType.DMA((2, 3, count)),
             pltpu.SemaphoreType.DMA((3, count)),
             pltpu.SemaphoreType.DMA((3, count)),
         ],

time: 23.5 us -> 23.4 us (level)
  no operation moved by 1% of the time
where the time goes in v8:
time: 23.4 us; the launch traced here: 23.2 us
  Pallas kernels  22.6 us (97%)
  between operations  0.64 us (3%)
    pallas_call x1, Pallas kernels, shards(): pl.pallas_call(functools.partial(local_kernel, sizes, count, chords, span...  20.9 us
    pallas_call x1, Pallas kernels, shards(): pl.pallas_call(write_kernel, in_specs=[vmem, vmem], out_specs=[hbm, hbm],...  1.68 us

profile of v8, /device:TPU:9, one launch (start us, length us, event | category | flops | bytes accessed | tf_op | source)
XLA Modules:
  0.0 23.2 jit_solution(4534786366657502079)
XLA Ops:
  0.6 20.9 %shard_map.30 = (f32[125,8,128]{2,1,0:T(8,128)S(1)}, f32[5,125,8,128]{3,2,1,0:T(8,128)S(1)}) custom-call(f32[5,125,8,128]{3,2,1,0:T(8,128)} %bitcast.3), custom_call_target="tpu_custom_call" | custom-call | tf_op jit(solution)/shard_map/pallas_call | solution.py:698
  21.6 1.7 %shard_map.31 = (f32[125,8,128]{2,1,0:T(8,128)}, f32[5,125,8,128]{3,2,1,0:T(8,128)}) custom-call(f32[125,8,128]{2,1,0:T(8,128)S(1)} %get-tuple-element.6.nu, f32[5,125,8,128]{3,2,1,0:T(8,128)S(1)} %get-tuple-element.7.residual), custom_call_target="tpu_custom_call" | custom-call | tf_op jit(solution)/shard_map/pallas_call | solution.py:732

commit v9 on v8

--- a/solution.py
+++ b/solution.py
@@ -362,7 +362,7 @@
     def onward(stage, k, v, route):
         return pltpu.make_async_remote_copy(
             src_ref=relay.at[route[4], v], dst_ref=lands[stage][k].at[v],
-            send_sem=pass_sem.at[route[4], v], recv_sem=recv_sem.at[stage, k, v],
+            send_sem=pass_sem.at[route[4]], recv_sem=recv_sem.at[stage, k, v],
             device_id=(ends[k][1], mate(route[1])), device_id_type=mesh_id,
         )
 
@@ -391,9 +391,16 @@
         each_relay(stage, variables, hand_on)
 
     def forwarded(stage):
-        each_relay(
-            stage, range(count), lambda k, v, route: onward(stage, k, v, route).wait_send()
-        )
+        def drained(k, v, route):
+            if v == route[2]:
+                sent_on = relay.at[route[4], pl.ds(v, route[3] - v)]
+                pltpu.make_async_remote_copy(
+                    src_ref=sent_on, dst_ref=sent_on, send_sem=pass_sem.at[route[4]],
+                    recv_sem=relay_sem.at[route[4], v],
+                    device_id=(ends[k][1], mate(route[1])), device_id_type=mesh_id,
+                ).wait_send()
+
+        each_relay(stage, range(count), drained)
 
     def launch(stage, axis, v):
         for k in (2 * axis, 2 * axis + 1):
@@ -722,7 +729,7 @@
             pltpu.SemaphoreType.DMA((2, 4)),
             pltpu.SemaphoreType.DMA((2, 3, count)),
             pltpu.SemaphoreType.DMA((3, count)),
-            pltpu.SemaphoreType.DMA((3, count)),
+            pltpu.SemaphoreType.DMA((3,)),
         ],
         compiler_params=pltpu.CompilerParams(
             collective_id=0, has_side_effects=True, vmem_limit_bytes=VMEM_BYTES

time: 23.4 us -> 23.3 us (level)
  no operation moved by 1% of the time
where the time goes in v9:
time: 23.3 us; the launch traced here: 23.1 us
  Pallas kernels  22.5 us (97%)
  between operations  0.64 us (3%)
    pallas_call x1, Pallas kernels, shards(): pl.pallas_call(functools.partial(local_kernel, sizes, count, chords, span...  20.8 us
    pallas_call x1, Pallas kernels, shards(): pl.pallas_call(write_kernel, in_specs=[vmem, vmem], out_specs=[hbm, hbm],...  1.68 us

profile of v9, /device:TPU:9, one launch (start us, length us, event | category | flops | bytes accessed | tf_op | source)
XLA Modules:
  0.0 23.1 jit_solution(6188891625897670306)
XLA Ops:
  0.6 20.8 %shard_map.30 = (f32[125,8,128]{2,1,0:T(8,128)S(1)}, f32[5,125,8,128]{3,2,1,0:T(8,128)S(1)}) custom-call(f32[5,125,8,128]{3,2,1,0:T(8,128)} %bitcast.3), custom_call_target="tpu_custom_call" | custom-call | tf_op jit(solution)/shard_map/pallas_call | solution.py:705
  21.4 1.7 %shard_map.31 = (f32[125,8,128]{2,1,0:T(8,128)}, f32[5,125,8,128]{3,2,1,0:T(8,128)}) custom-call(f32[125,8,128]{2,1,0:T(8,128)S(1)} %get-tuple-element.6.nu, f32[5,125,8,128]{3,2,1,0:T(8,128)S(1)} %get-tuple-element.7.residual), custom_call_target="tpu_custom_call" | custom-call | tf_op jit(solution)/shard_map/pallas_call | solution.py:739
